TPU v7x, 32 devices: a whole 2x2x4 slice. The times are simulated.
32 devices in a mesh: dp: 2 (over core), row: 4 (over y, x), col: 4 (over z).
Axes of the slice: x: 2, y: 2, z: 4, core: 2. Of those that a mesh axis runs over, the one named last changes fastest.
Arguments:
- block_input: float32 [4096, 2048], P(('dp', 'row'), 'col'), as said below
- out_grad: float32 [4096, 2048], P(('dp', 'row'), 'col'), may hold values from -6 to 6
- ln1_gain: float32 [2048], P('col'), may hold values from 0.25 to 1.75
- ln1_bias: float32 [2048], P('col'), may hold values from -1.75 to 1.75
- ln2_gain: float32 [2048], P('col'), may hold values from 0.25 to 1.75
- ln2_bias: float32 [2048], P('col'), may hold values from -1.75 to 1.75
- w_qkv: bfloat16 [2048, 6144], P('row', 'col'), as said below
- b_qkv: float32 [6144], P('col'), may hold values from -3 to 3
- w_dense: bfloat16 [2048, 2048], P('col', 'row'), may hold values from -0.5 to 0.5
- b_dense: float32 [2048], P('col'), may hold values from -1.75 to 1.75
- w_fc: bfloat16 [2048, 8192], P('row', 'col'), may hold values from -0.125 to 0.125
- b_fc: float32 [8192], P('col'), may hold values from -3 to 3
- w_proj: bfloat16 [8192, 2048], P('col', 'row'), may hold values from -0.0625 to 0.0625
- b_proj: float32 [2048], P('col'), may hold values from -1.75 to 1.75
Outputs:
- block_output: float32 [4096, 2048], P(('dp', 'row'), 'col')
- input_grad: float32 [4096, 2048], P(('dp', 'row'), 'col')
- grad_ln1_gain: float32 [2048], P('col')
- grad_ln1_bias: float32 [2048], P('col')
- grad_ln2_gain: float32 [2048], P('col')
- grad_ln2_bias: float32 [2048], P('col')
- grad_w_qkv: float32 [2048, 6144], P('row', 'col')
- grad_b_qkv: float32 [6144], P('col')
- grad_w_dense: float32 [2048, 2048], P('col', 'row')
- grad_b_dense: float32 [2048], P('col')
- grad_w_fc: float32 [2048, 8192], P('row', 'col')
- grad_b_fc: float32 [8192], P('col')
- grad_w_proj: float32 [8192, 2048], P('col', 'row')
- grad_b_proj: float32 [2048], P('col')
Inputs may be any that keep to these rules, and one draw needn't show every extreme that they name: `block_input`: finite real values. `w_qkv`: finite real values.
All inputs are finite; a program needn't handle non-finite values.
Results may differ from a plain program's by a relative error of at most 0.011.
Values may be sent and summed in bfloat16 or wider, within the bound.
A program may use at most 320 MiB of HBM per device.

v0:
```python
import math

import jax
import jax.numpy as jnp
from jax import lax
from jax.sharding import PartitionSpec as P

D = 2048
HD = 256
ROT = 64
SEQ = 512


epsilon = 1e-05
contract_last = (((1,), (1,)), ((), ()))
contract_first = (((0,), (0,)), ((), ()))


def angle_tables(length):
    half_rot = ROT // 2
    position = jnp.arange(length, dtype=jnp.float32)
    exponent = jnp.arange(half_rot, dtype=jnp.float32) * (2.0 / ROT)
    frequency = 10000.0 ** (-exponent)
    angles = position[:, None] * frequency[None, :]
    return (jnp.cos(angles), jnp.sin(angles))


def rotate_fwd(values, cosine, sine_vals):
    half_rot = ROT // 2
    first = values[..., :half_rot]
    second = values[..., half_rot:ROT]
    cos_part = cosine[:, None, :]
    sin_part = sine_vals[:, None, :]
    return jnp.concatenate(
        [
            first * cos_part - second * sin_part,
            second * cos_part + first * sin_part,
            values[..., ROT:],
        ],
        axis=-1,
    )


def rotate_back(grads, cosine, sine_vals):
    half_rot = ROT // 2
    first = grads[..., :half_rot]
    second = grads[..., half_rot:ROT]
    cos_part = cosine[:, None, :]
    sin_part = sine_vals[:, None, :]
    return jnp.concatenate(
        [
            first * cos_part + second * sin_part,
            second * cos_part - first * sin_part,
            grads[..., ROT:],
        ],
        axis=-1,
    )


def gelu_value(pre_act):
    return 0.5 * pre_act * (1.0 + lax.erf(pre_act * 0.7071067811865476))


def gelu_slope(pre_act):
    return 0.5 * (
        1.0 + lax.erf(pre_act * 0.7071067811865476)
    ) + pre_act * 0.3989422804014327 * jnp.exp(-0.5 * pre_act * pre_act)


def shards(
    block_input,
    out_grad,
    ln1_gain,
    ln1_bias,
    ln2_gain,
    ln2_bias,
    w_qkv,
    b_qkv,
    w_dense,
    b_dense,
    w_fc,
    b_fc,
    w_proj,
    b_proj,
):
    tok_rows = block_input.shape[0]
    seq_count = tok_rows // SEQ
    qkv_cols = w_qkv.shape[1]
    fc_cols = w_fc.shape[1]
    local_heads = qkv_cols // (3 * HD)
    head_cols = local_heads * HD
    scale = 1.0 / math.sqrt(HD)
    cosine, sine_vals = angle_tables(SEQ)
    causal = jnp.arange(SEQ)[:, None] >= jnp.arange(SEQ)[None, :]
    row_total, square_total = lax.psum(
        (jnp.sum(block_input, axis=1), jnp.sum(block_input * block_input, axis=1)), "col"
    )
    mean_row = (row_total / D)[:, None]
    var_row = (square_total / D)[:, None] - mean_row * mean_row
    inv_std = lax.rsqrt(var_row + epsilon)
    x_hat = (block_input - mean_row) * inv_std
    normed_one = (x_hat * ln1_gain + ln1_bias).astype(jnp.bfloat16)
    normed_two = (x_hat * ln2_gain + ln2_bias).astype(jnp.bfloat16)
    wide_one, wide_two = (
        lax.all_gather(normed_one, "col", axis=1, tiled=True),
        lax.all_gather(normed_two, "col", axis=1, tiled=True),
    )
    part_one = wide_one
    part_two = wide_two
    qkv_pre = jnp.dot(
        part_one,
        lax.all_gather(w_qkv, "row", axis=0, tiled=True),
        preferred_element_type=jnp.float32,
    )
    fc_pre = jnp.dot(
        part_two,
        lax.all_gather(w_fc, "row", axis=0, tiled=True),
        preferred_element_type=jnp.float32,
    )
    qkv_pre = qkv_pre + b_qkv
    fc_pre = fc_pre + b_fc

    def forward_seq(block):
        query = rotate_fwd(block[:, :, 0], cosine, sine_vals).astype(jnp.bfloat16)
        keys = rotate_fwd(block[:, :, 1], cosine, sine_vals).astype(jnp.bfloat16)
        values = block[:, :, 2].astype(jnp.bfloat16)
        scores = jnp.einsum("qhd,khd->hqk", query, keys, preferred_element_type=jnp.float32) * scale
        masked = jnp.where(causal[None], scores, -1e30)
        row_max = jnp.max(masked, axis=-1, keepdims=True)
        exp_sum = jnp.sum(
            jnp.where(causal[None], jnp.exp(masked - row_max), 0.0), axis=-1, keepdims=True
        )
        log_total = row_max + jnp.log(exp_sum)
        probs_low = jnp.where(causal[None], jnp.exp(masked - log_total), 0.0).astype(jnp.bfloat16)
        attended = jnp.einsum(
            "hqk,khd->qhd", probs_low, values, preferred_element_type=jnp.float32
        ).astype(jnp.bfloat16)
        return (query, keys, values, attended, log_total)

    query, keys, values, attended, log_total = lax.map(
        forward_seq, qkv_pre.reshape(seq_count, SEQ, local_heads, 3, HD)
    )
    attn_out = attended.reshape(tok_rows, head_cols)
    gelu_out = gelu_value(fc_pre).astype(jnp.bfloat16)
    out_stack = jnp.concatenate([w_dense, w_proj], axis=0)
    shard_piece = lax.all_gather(out_stack, "row", axis=1, tiled=True)
    mixed = jnp.dot(
        attn_out, shard_piece[:head_cols], preferred_element_type=jnp.float32
    ) + jnp.dot(gelu_out, shard_piece[head_cols:], preferred_element_type=jnp.float32)
    branch_sum = lax.psum_scatter(mixed, "col", scatter_dimension=1, tiled=True)
    block_output = block_input + branch_sum + b_dense + b_proj
    grad_low = out_grad.astype(jnp.bfloat16)
    wide_grad = lax.all_gather(grad_low, "col", axis=1, tiled=True)
    both_grad = lax.dot_general(
        wide_grad,
        lax.all_gather(out_stack, "row", axis=1, tiled=True),
        contract_last,
        preferred_element_type=jnp.float32,
    )
    attn_grad = both_grad[:, :head_cols]
    gelu_grad = both_grad[:, head_cols:]
    attn_grad_low = attn_grad.astype(jnp.bfloat16)
    fc_grad = gelu_grad * gelu_slope(fc_pre)
    fc_bias_grad = jnp.sum(fc_grad, axis=0)
    fc_grad_low = fc_grad.astype(jnp.bfloat16)

    def backward_seq(items):
        query_s, keys_s, values_s, attended_s, log_s, head_grad = items
        scores = (
            jnp.einsum("qhd,khd->hqk", query_s, keys_s, preferred_element_type=jnp.float32) * scale
        )
        probs = jnp.where(
            causal[None], jnp.exp(jnp.where(causal[None], scores, -1e30) - log_s), 0.0
        )
        probs_low = probs.astype(jnp.bfloat16)
        value_grad = jnp.einsum(
            "hqk,qhd->khd", probs_low, head_grad, preferred_element_type=jnp.float32
        )
        prob_grad = jnp.einsum(
            "qhd,khd->hqk", head_grad, values_s, preferred_element_type=jnp.float32
        )
        delta_row = jnp.transpose(
            jnp.sum(head_grad.astype(jnp.float32) * attended_s.astype(jnp.float32), axis=-1), (1, 0)
        )[:, :, None]
        score_grad = (probs * (prob_grad - delta_row) * scale).astype(jnp.bfloat16)
        query_grad = jnp.einsum(
            "hqk,khd->qhd", score_grad, keys_s, preferred_element_type=jnp.float32
        )
        key_grad = jnp.einsum(
            "hqk,qhd->khd", score_grad, query_s, preferred_element_type=jnp.float32
        )
        return jnp.stack(
            [
                rotate_back(query_grad, cosine, sine_vals),
                rotate_back(key_grad, cosine, sine_vals),
                value_grad,
            ],
            axis=2,
        )

    head_grads = attn_grad_low.reshape(seq_count, SEQ, local_heads, HD)
    qkv_grad = lax.map(
        backward_seq, (query, keys, values, attended, log_total, head_grads)
    ).reshape(tok_rows, qkv_cols)
    qkv_bias_grad = jnp.sum(qkv_grad, axis=0)
    qkv_grad_low = qkv_grad.astype(jnp.bfloat16)
    in_stack = jnp.concatenate([w_qkv, w_fc], axis=1)
    shard_piece = lax.all_gather(in_stack, "row", axis=0, tiled=True)
    norm_grads = jnp.stack(
        [
            lax.dot_general(
                qkv_grad_low,
                shard_piece[:, :qkv_cols],
                contract_last,
                preferred_element_type=jnp.float32,
            ),
            lax.dot_general(
                fc_grad_low,
                shard_piece[:, qkv_cols:],
                contract_last,
                preferred_element_type=jnp.float32,
            ),
        ]
    )
    part_one = wide_one
    part_two = wide_two
    row_part = lax.psum_scatter(
        jnp.concatenate(
            [
                lax.dot_general(
                    part_one, qkv_grad_low, contract_first, preferred_element_type=jnp.float32
                ),
                lax.dot_general(
                    part_two, fc_grad_low, contract_first, preferred_element_type=jnp.float32
                ),
                lax.dot_general(
                    wide_grad, attn_out, contract_first, preferred_element_type=jnp.float32
                ),
                lax.dot_general(
                    wide_grad, gelu_out, contract_first, preferred_element_type=jnp.float32
                ),
            ],
            axis=1,
        ),
        "row",
        scatter_dimension=0,
        tiled=True,
    )
    grad_rows = lax.psum(row_part, "dp")
    qkv_total = grad_rows[:, :qkv_cols]
    fc_total = grad_rows[:, qkv_cols : qkv_cols + fc_cols]
    dense_total = grad_rows[:, qkv_cols + fc_cols : qkv_cols + fc_cols + head_cols].T
    proj_total = grad_rows[:, qkv_cols + fc_cols + head_cols :].T
    norm_local = lax.psum_scatter(norm_grads, "col", scatter_dimension=2, tiled=True)
    grad_one = norm_local[0]
    grad_two = norm_local[1]
    hat_grad = grad_one * ln1_gain + grad_two * ln2_gain
    total_hat, total_cross = lax.psum(
        (jnp.sum(hat_grad, axis=1), jnp.sum(hat_grad * x_hat, axis=1)), "col"
    )
    input_grad = out_grad + inv_std * (
        hat_grad - (total_hat / D)[:, None] - x_hat * (total_cross / D)[:, None]
    )
    gain_one, shift_one, gain_two, shift_two, qkv_bias_total, fc_bias_total, out_bias_total = (
        lax.psum(
            (
                jnp.sum(grad_one * x_hat, axis=0),
                jnp.sum(grad_one, axis=0),
                jnp.sum(grad_two * x_hat, axis=0),
                jnp.sum(grad_two, axis=0),
                qkv_bias_grad,
                fc_bias_grad,
                jnp.sum(out_grad, axis=0),
            ),
            ("dp", "row"),
        )
    )
    return (
        block_output,
        input_grad,
        gain_one,
        shift_one,
        gain_two,
        shift_two,
        qkv_total,
        qkv_bias_total,
        dense_total,
        out_bias_total,
        fc_total,
        fc_bias_total,
        proj_total,
        out_bias_total,
    )


def solution(mesh):
    return jax.shard_map(
        shards,
        mesh=mesh,
        in_specs=(
            P(("dp", "row"), "col"),
            P(("dp", "row"), "col"),
            P("col"),
            P("col"),
            P("col"),
            P("col"),
            P("row", "col"),
            P("col"),
            P("col", "row"),
            P("col"),
            P("row", "col"),
            P("col"),
            P("col", "row"),
            P("col"),
        ),
        out_specs=(
            P(("dp", "row"), "col"),
            P(("dp", "row"), "col"),
            P("col"),
            P("col"),
            P("col"),
            P("col"),
            P("row", "col"),
            P("col"),
            P("col", "row"),
            P("col"),
            P("row", "col"),
            P("col"),
            P("col", "row"),
            P("col"),
        ),
        check_vma=False,
    )
```

profile of v0, /device:TPU:1, one launch (start us, length us, event | category | flops | bytes accessed | tf_op | source)
XLA Modules:
  0.0 1304.7 jit_solution(7486907103567437499)
XLA Ops:
  8.9 10.8 all-reduce.2
  24.6 3.4 pad_maximum_fusion.4
  29.2 3.7 pad_maximum_fusion.2
  35.4 32.7 %all-gather.8.cloned.1.call-done = bf16[512,2048]{1,0:T(8,128)(2,1)} async-done(((bf16[512,512]{1,0:T(8,128)(2,1)}), bf16[512,2048]{1,0:T(8,128)(2,1)}) %all-gather.8.cloned.1.call-update) | async-done | bytes 2097168 | tf_op jit(solution)/shard_map/all_gather | solution.py:105
  68.2 70.7 %all-gather.10.cloned.1.call-done = bf16[2048,1536]{1,0:T(8,128)(2,1)} async-done(((bf16[512,1536]{1,0:T(8,128)(2,1)}), bf16[2048,1536]{1,0:T(8,128)(2,1)}) %all-gather.10.cloned.1.call-update) | async-done | bytes 6291472 | tf_op jit(solution)/shard_map/all_gather | solution.py:112
  138.9 8.5 convolution_add_fusion.1
  165.6 21.1 %all-gather.18.cloned.1.call-done = bf16[512,2048]{1,0:T(8,128)(2,1)} async-done(((bf16[512,512]{1,0:T(8,128)(2,1)}), bf16[512,2048]{1,0:T(8,128)(2,1)}) %all-gather.18.cloned.1.call-update) | async-done | bytes 2097168 | tf_op jit(solution)/shard_map/all_gather | solution.py:153
  186.7 105.9 %all-gather.12.cloned.1.call-done = bf16[2560,2048]{1,0:T(8,128)(2,1)} async-done(((bf16[2560,512]{1,0:T(8,128)(2,1)}), bf16[2560,2048]{1,0:T(8,128)(2,1)}) %all-gather.12.cloned.1.call-update) | async-done | bytes 10485776 | tf_op jit(solution)/shard_map/all_gather | solution.py:146
  292.6 9.2 convolution_bitcast_fusion.1
  307.1 3.4 multiply_reduce_fusion.1
  320.6 5.0 convolution_bitcast_fusion.2
  325.6 6.3 fusion.42
  332.0 7.7 all-gather.14.cloned.1.call-done
  339.7 88.0 %all-gather.16.cloned.1.call-done = bf16[2048,2048]{1,0:T(8,128)(2,1)} async-done(((bf16[512,2048]{1,0:T(8,128)(2,1)}), bf16[2048,2048]{1,0:T(8,128)(2,1)}) %all-gather.16.cloned.1.call-update) | async-done | bytes 8388624 | tf_op jit(solution)/shard_map/all_gather | solution.py:117
  427.7 9.9 fusion.36
  437.7 9.4 fusion.23
  447.6 8.3 convolution_bitcast_fusion
  455.9 32.8 %pad_maximum_fusion = f32[2048,6144]{0,1:T(8,128)} fusion(f32[2048,2048]{0,1:T(8,128)} %convolution_bitcast_fusion, f32[2048,512]{0,1:T(8,128)S(1)} %copy-done, f32[2048,2048]{0,1:T(8,128)} %fusion.23, f32[2048,1536]{0,1:T(8,128)} %fusion.42), kind=kLoop, calls=%fused_computation | loop fusion | flops 37748736 | bytes 100663296 | tf_op jit(solution)/shard_map/concatenate | solution.py:228
  488.8 80.6 %all-gather.20.cloned.1.call-done = bf16[2048,3584]{1,0:T(8,128)(2,1)} async-done(((bf16[512,3584]{1,0:T(8,128)(2,1)}), bf16[2048,3584]{1,0:T(8,128)(2,1)}) %all-gather.20.cloned.1.call-update) | async-done | bytes 14680080 | tf_op jit(solution)/shard_map/all_gather | solution.py:208
  569.4 6.2 fusion.10
  575.7 7.0 fusion.13
  582.7 3.8 pad_maximum_fusion.1
  586.8 9.4 fusion.2
  596.2 5.0 convolution_add_fusion
  601.3 395.2 %reduce-scatter.8.cloned.1.call-done = f32[512,6144]{0,1:T(8,128)} async-done(((f32[2048,6144]{0,1:T(8,128)}), f32[512,6144]{0,1:T(8,128)}) %reduce-scatter.8.cloned.1.call-update) | async-done | bytes 12582928 | tf_op jit(solution)/shard_map/reduce_scatter | solution.py:227
  998.2 145.1 %reduce-scatter.6.cloned.1.call-done = f32[2,512,512]{2,1,0:T(8,128)} async-done(((f32[2,512,2048]{2,1,0:T(8,128)}), f32[2,512,512]{2,1,0:T(8,128)}) %reduce-scatter.6.cloned.1.call-update) | async-done | bytes 2097168 | tf_op jit(solution)/shard_map/reduce_scatter | solution.py:254
  1147.3 28.6 %all-reduce = (f32[512]{0:T(512)}, f32[512]{0:T(512)}, f32[512]{0:T(512)}, f32[512]{0:T(512)}, f32[1536]{0:T(1024)}, /*index=5*/f32[512]{0:T(512)S(1)}, f32[2048]{0:T(1024)}) all-reduce(f32[512]{0:T(512)S(1)} %get-tuple-element.120, f32[512]{0:T(512)S(1)} %get-tuple-element.122, ...), channel_id=1, replica_groups=mesh['dp'=2,'row'=4,'col'=4] {'dp','row'}, use_global_device_ids=true, to_apply=%region_14.15 | all-reduce | flops 6144 | bytes 49152 | tf_op jit(solution)/shard_map/psum | solution.py:265
  1175.9 11.4 all-reduce.1
  1187.3 36.5 %reduce-scatter.4.cloned.1.call-done = f32[512,512]{1,0:T(8,128)} async-done(((f32[512,2048]{1,0:T(8,128)}), f32[512,512]{1,0:T(8,128)}) %reduce-scatter.4.cloned.1.call-update) | async-done | bytes 1048592 | tf_op jit(solution)/shard_map/reduce_scatter | solution.py:150
  1226.7 50.9 %all-reduce.5.cloned.1.call-done = f32[512,6144]{0,1:T(8,128)} async-done(((f32[512,6144]{0,1:T(8,128)}), f32[512,6144]{0,1:T(8,128)}) %all-reduce.5.cloned.1.call-update) | async-done | bytes 12582928 | tf_op jit(solution)/shard_map/psum | solution.py:249
  1281.8 7.7 slice_bitcast_fusion
  1289.6 5.3 copy.89
  (156 shorter events, 60.1 us)
Async XLA Ops:
  7.2 15.9 %copy-start.6 = (f32[512,512]{1,0:T(8,128)S(1)}, f32[512,512]{1,0:T(8,128)}, u32[]{:S(2)}) copy-start(f32[512,512]{1,0:T(8,128)} %param.15) | copy-start | bytes 3145732
  7.2 17.4 %copy-start.27 = (bf16[512,512]{1,0:T(8,128)(2,1)S(1)}, bf16[512,512]{1,0:T(8,128)(2,1)}, u32[]{:S(2)}) copy-start(bf16[512,512]{1,0:T(8,128)(2,1)} %param.22) | copy-start | bytes 1572868
  7.2 61.0 %all-gather.8.cloned.1.call-start = ((), (), s32[]{:S(2)}) async-start(), calls=%async_computation.3 | async-start | bytes 2621440 | tf_op jit(solution)/shard_map/all_gather | solution.py:105
  22.2 116.6 %all-gather.10.cloned.1.call-start = ((), (), s32[]{:S(2)}) async-start(), calls=%async_computation.4 | async-start | bytes 7864320 | tf_op jit(solution)/shard_map/all_gather | solution.py:112
  23.0 163.7 %all-gather.18.cloned.1.call-start = ((), (), s32[]{:S(2)}) async-start(), calls=%async_computation.9 | async-start | bytes 2621440 | tf_op jit(solution)/shard_map/all_gather | solution.py:153
  24.5 268.1 %all-gather.12.cloned.1.call-start = ((), (), s32[]{:S(2)}) async-start(), calls=%async_computation.5 | async-start | bytes 13107200 | tf_op jit(solution)/shard_map/all_gather | solution.py:146
  28.0 311.7 %all-gather.14.cloned.1.call-start = ((), (), s32[]{:S(2)}) async-start(), calls=%async_computation.6 | async-start | bytes 2621440 | tf_op jit(solution)/shard_map/all_gather | solution.py:106
  28.6 399.1 %all-gather.16.cloned.1.call-start = ((), (), s32[]{:S(2)}) async-start(), calls=%async_computation.7 | async-start | bytes 10485760 | tf_op jit(solution)/shard_map/all_gather | solution.py:117
  29.2 109.7 %copy-start.41 = (f32[1536]{0:T(1024)S(1)}, f32[1536]{0:T(1024)}, u32[]{:S(2)}) copy-start(f32[1536]{0:T(1024)} %param.21) | copy-start | bytes 18436
  29.2 540.2 %all-gather.20.cloned.1.call-start = ((), (), s32[]{:S(2)}) async-start(), calls=%async_computation.10 | async-start | bytes 18350080 | tf_op jit(solution)/shard_map/all_gather | solution.py:208
  32.9 963.6 %reduce-scatter.8.cloned.1.call-start = ((), (), s32[]{:S(2)}) async-start(), calls=%async_computation.12 | async-start | bytes 62914560 | tf_op jit(solution)/shard_map/reduce_scatter | solution.py:227
  320.6 5.0 copy-start.39
  325.6 102.1 %copy-start.42 = (f32[2048]{0:T(1024)S(1)}, f32[2048]{0:T(1024)}, u32[]{:S(2)}) copy-start(f32[2048]{0:T(1024)} %param.25) | copy-start | bytes 24580
  427.7 9.9 copy-start.40
  437.6 9.5 copy-start.43
  437.6 10.0 copy-start.45
  437.7 10.0 copy-start.13
  447.6 8.3 copy-start
  488.7 654.6 %reduce-scatter.6.cloned.1.call-start = ((), (), s32[]{:S(2)}) async-start(), calls=%async_computation.11 | async-start | bytes 10485760 | tf_op jit(solution)/shard_map/reduce_scatter | solution.py:254
  569.4 6.2 copy-start.44
  586.5 637.3 %reduce-scatter.4.cloned.1.call-start = ((), (), s32[]{:S(2)}) async-start(), calls=%async_computation.8 | async-start | bytes 5242880 | tf_op jit(solution)/shard_map/reduce_scatter | solution.py:150
  601.2 676.3 %all-reduce.5.cloned.1.call-start = ((), (), s32[]{:S(2)}) async-start(), calls=%async_computation.13 | async-start | bytes 25165824 | tf_op jit(solution)/shard_map/psum | solution.py:249
  996.5 148.5 %copy-start.1 = (f32[512,512]{1,0:T(8,128)S(1)}, f32[512,512]{1,0:T(8,128)}, u32[]{:S(2)}) copy-start(f32[512,512]{1,0:T(8,128)} %param.14) | copy-start | bytes 3145732
  996.6 148.4 %copy-start.30 = (f32[512]{0:T(512)S(1)}, f32[512]{0:T(512)}, u32[]{:S(2)}) copy-start(f32[512]{0:T(512)} %copy-done.29) | copy-start | bytes 6148
  996.6 148.4 %copy-start.32 = (f32[512]{0:T(512)S(1)}, f32[512]{0:T(512)}, u32[]{:S(2)}) copy-start(f32[512]{0:T(512)} %copy-done.31) | copy-start | bytes 6148
  996.6 148.4 %copy-start.34 = (f32[512]{0:T(512)S(1)}, f32[512]{0:T(512)}, u32[]{:S(2)}) copy-start(f32[512]{0:T(512)} %param.16) | copy-start | bytes 6148
  996.6 148.4 %copy-start.35 = (f32[512]{0:T(512)S(1)}, f32[512]{0:T(512)}, u32[]{:S(2)}) copy-start(f32[512]{0:T(512)} %param.18) | copy-start | bytes 6148
  996.6 150.7 %copy-start.33 = (f32[512]{0:T(512)S(1)}, f32[512]{0:T(512)}, u32[]{:S(2)}) copy-start(f32[512]{0:T(512)} %get-tuple-element.155) | copy-start | bytes 6148
  996.6 227.2 %copy-start.36 = (f32[512]{0:T(512)S(1)}, f32[512]{0:T(512)}, u32[]{:S(2)}) copy-start(f32[512]{0:T(512)} %param.27) | copy-start | bytes 6148
  996.6 227.2 %copy-start.37 = (f32[512]{0:T(512)S(1)}, f32[512]{0:T(512)}, u32[]{:S(2)}) copy-start(f32[512]{0:T(512)} %param.23) | copy-start | bytes 6148
  998.1 225.7 %copy-start.7 = (f32[512,512]{1,0:T(8,128)S(1)}, f32[512,512]{1,0:T(8,128)}, u32[]{:S(2)}) copy-start(f32[512,512]{1,0:T(8,128)} %param.15) | copy-start | bytes 3145732
  1175.9 121.3 %copy-start.38 = (f32[512]{0:T(512)}, f32[512]{0:T(512)S(1)}, u32[]{:S(2)}) copy-start(f32[512]{0:T(512)S(1)} %get-tuple-element.204) | copy-start | bytes 6148
  (26 other events, 85.6 us)
Sparse Core Ops, SparseCore 0:
  22.4 45.7 all-gather.7
  70.0 68.8 all-gather.9
  141.0 45.6 all-gather.17
  189.0 103.5 all-gather.11
  294.0 45.6 all-gather.13
  341.4 86.2 all-gather.15
  429.6 139.8 all-gather.19
  572.5 423.9 reduce-scatter.7
  998.9 144.3 reduce-scatter.5
  1146.0 77.7 reduce-scatter.3
  1226.3 51.2 all-reduce.4
where the time goes:
time: 1310 us; the launch traced here: 1300 us
  waiting for transfers between devices  1040 us (79%)
  matrix products  91.8 us (7%)
  other arithmetic  65.9 us (5%)
  blocking collectives  50.8 us (4%)
  local copies, waits for them, and re-layouts  44.2 us (3%)
  between operations  14.9 us (1%)
    reduce_scatter x1, waiting for transfers between devices, shards(): lax.psum_scatter(jnp.concatenate([lax.dot_general(part_one, qkv_grad_low,...  395 us
    reduce_scatter x1, waiting for transfers between devices, shards(): lax.psum_scatter(norm_grads, 'col', scatter_dimension=2, tiled=True)  145 us
    all_gather x1, waiting for transfers between devices, shards(): shard_piece = lax.all_gather(out_stack, 'row', axis=1, tiled=True)  106 us
    all_gather x1, waiting for transfers between devices, shards(): lax.all_gather(w_fc, 'row', axis=0, tiled=True)  88 us
    all_gather x1, waiting for transfers between devices, shards(): shard_piece = lax.all_gather(in_stack, 'row', axis=0, tiled=True)  80.6 us
    all_gather x1, waiting for transfers between devices, shards(): lax.all_gather(w_qkv, 'row', axis=0, tiled=True)  70.7 us
    psum x1, waiting for transfers between devices, shards(): grad_rows = lax.psum(row_part, 'dp')  50.9 us
    reduce_scatter x1, waiting for transfers between devices, shards(): branch_sum = lax.psum_scatter(mixed, 'col', scatter_dimension=1, tiled=True)  36.5 us
  transfers between devices with their start and end apart: 11, of which 11 were waited for; matrix products, arithmetic and copies ran while one was open for 13% of the time, Pallas kernels for 0%

commit v1 on v0

--- a/solution.py
+++ b/solution.py
@@ -1,8 +1,12 @@
+import functools
 import math
 
 import jax
 import jax.numpy as jnp
+import numpy as np
 from jax import lax
+from jax.experimental import pallas as pl
+from jax.experimental.pallas import tpu as pltpu
 from jax.sharding import PartitionSpec as P
 
 D = 2048
@@ -293,9 +297,860 @@
     )
 
 
+f32 = jnp.float32
+bf16 = jnp.bfloat16
+MESH = pl.DeviceIdType.MESH
+VMEM = pltpu.VMEM
+Q = 256
+HALF = 4 * Q
+
+
+def flip(a, b):
+    return a + b - 2 * a * b
+
+
+def span(start, size):
+    return pl.ds(pl.multiple_of(start, size), size)
+
+
+def mm(a, b):
+    return jnp.dot(a, b, preferred_element_type=f32)
+
+
+def mm_nt(a, b):
+    return lax.dot_general(a, b, (((1,), (1,)), ((), ())), preferred_element_type=f32)
+
+
+def mm_tn(a, b):
+    return lax.dot_general(a, b, (((0,), (0,)), ((), ())), preferred_element_type=f32)
+
+
+class Net:
+    def __init__(self, send_sems, recv_sems, local_sems):
+        self.k = lax.axis_index("dp")
+        self.r = lax.axis_index("row")
+        self.c = lax.axis_index("col")
+        k, r, c = self.k, self.r, self.c
+        self.core = (1 - k, r, c)
+        self.x = (k, r + 1 - 2 * (r % 2), c)
+        self.y = (k, r + 2 - 4 * (r // 2), c)
+        near = c + 1 - 2 * (c % 2)
+        self.z = (None, (k, r, near), (k, r, c + 2 - 4 * (c // 2)), (k, r, 3 - c))
+        self.middle = flip(c % 2, c // 2) == 1
+        self.send_sems, self.recv_sems, self.local_sems = send_sems, recv_sems, local_sems
+        self.remote_count = 0
+        self.local_count = 0
+        self.pending = []
+
+    def mix(self, j):
+        return flip(j % 2, flip(self.c % 2, self.r % 2)) + 2 * flip(
+            j // 2, flip(self.c // 2, self.r // 2)
+        )
+
+    def barrier(self):
+        sem = pltpu.get_barrier_semaphore()
+        peers = (self.core, self.x, self.y) + self.z[1:]
+        for peer in peers:
+            pl.semaphore_signal(sem, inc=1, device_id=peer, device_id_type=MESH)
+        pl.semaphore_wait(sem, len(peers))
+
+    def slot(self):
+        self.remote_count += 1
+        return self.remote_count - 1
+
+    def remote(self, src, dst, peer):
+        slot = self.slot()
+        copy = pltpu.make_async_remote_copy(
+            src_ref=src,
+            dst_ref=dst,
+            send_sem=self.send_sems.at[slot],
+            recv_sem=self.recv_sems.at[slot],
+            device_id=peer,
+            device_id_type=MESH,
+        )
+        copy.start()
+        self.pending.append(copy)
+        return copy
+
+    def local(self, src, dst):
+        copy = pltpu.make_async_copy(src, dst, self.local_sems.at[self.local_count])
+        self.local_count += 1
+        copy.start()
+        return copy
+
+    def drain(self):
+        for copy in self.pending:
+            copy.wait_send()
+
+
+class Gather:
+    def __init__(self, net, shard, full, by_rows):
+        self.net, self.shard, self.full, self.by_rows = net, shard, full, by_rows
+        self.depth = Q // 2 if by_rows else shard.shape[0] // 2
+        self.placed = []
+
+    def own(self, half, part=None):
+        if self.by_rows:
+            if part is None:
+                return self.shard.at[span(half * Q, Q), :]
+            return self.shard.at[span(half * Q + part * self.depth, self.depth), :]
+        rows = slice(None) if part is None else pl.ds(part * self.depth, self.depth)
+        return self.shard.at[rows, span(half * Q, Q)]
+
+    def chunk(self, s, i, part=None):
+        start = s * HALF + i * Q
+        if self.by_rows:
+            if part is None:
+                return self.full.at[pl.ds(start, Q), :]
+            return self.full.at[pl.ds(start + part * self.depth, self.depth), :]
+        rows = slice(None) if part is None else pl.ds(part * self.depth, self.depth)
+        return self.full.at[rows, pl.ds(start, Q)]
+
+    def place_own(self):
+        net = self.net
+        self.placed = [
+            net.local(self.own(net.k), self.chunk(0, 0)),
+            net.local(self.own(1 - net.k), self.chunk(1, 0)),
+        ]
+
+    def send_own(self):
+        net, k = self.net, self.net.k
+        self.y0 = net.remote(self.own(k, 0), self.chunk(0, 2, 0), net.y)
+        self.x1 = net.remote(self.own(k, 1), self.chunk(0, 1, 1), net.x)
+        self.y1 = net.remote(self.own(k, 1), self.chunk(0, 2, 1), net.y)
+        self.x0 = net.remote(self.own(k, 0), self.chunk(0, 1, 0), net.x)
+
+    def forward(self):
+        net = self.net
+        self.y0.wait_recv()
+        self.d0 = net.remote(self.chunk(0, 2, 0), self.chunk(0, 3, 0), net.x)
+        self.x1.wait_recv()
+        self.d1 = net.remote(self.chunk(0, 1, 1), self.chunk(0, 3, 1), net.y)
+
+    def swap_near(self):
+        net = self.net
+        self.x0.wait_recv()
+        self.c1 = net.remote(self.chunk(0, 1), self.chunk(1, 1), net.core)
+        self.y1.wait_recv()
+        self.c2 = net.remote(self.chunk(0, 2), self.chunk(1, 2), net.core)
+
+    def swap_far(self):
+        net = self.net
+        self.d0.wait_recv()
+        self.d1.wait_recv()
+        self.c3 = net.remote(self.chunk(0, 3), self.chunk(1, 3), net.core)
+
+    def ready(self):
+        for copy in (self.c1, self.c2, self.c3):
+            copy.wait_recv()
+        for copy in self.placed:
+            copy.wait()
+
+
+class Line:
+    def __init__(self, net, slots):
+        self.net, self.slots = net, slots
+        self.ids = [None] + [net.slot() for _ in range(3)]
+        self.sends = []
+
+    def copy(self, src, dst, peer, send):
+        net = self.net
+        return pltpu.make_async_remote_copy(
+            src_ref=self.slots.at[src],
+            dst_ref=self.slots.at[dst],
+            send_sem=net.send_sems.at[send],
+            recv_sem=net.recv_sems.at[self.ids[dst]],
+            device_id=peer,
+            device_id_type=MESH,
+        )
+
+    def start(self):
+        net = self.net
+        first = self.copy(0, 1, net.z[1], self.ids[1])
+        first.start()
+        net.pending.append(first)
+        self.hops = [
+            self.copy(0, 3, net.z[3], self.ids[2]),
+            self.copy(1, 2, net.z[3], self.ids[3]),
+            self.copy(3, 2, net.z[1], net.slot()),
+            self.copy(2, 3, net.z[1], net.slot()),
+        ]
+
+        @pl.when(net.middle)
+        def _():
+            self.hops[0].start()
+
+    def arrived(self, slot):
+        return self.copy(0, slot, self.net.z[1], self.ids[slot])
+
+    def step(self, number):
+        slot = (1, 3, 2)[number]
+
+        @pl.when(self.net.middle)
+        def _():
+            self.arrived(slot).wait_recv()
+            self.hops[number + 1].start()
+
+    def ready(self):
+        @pl.when(jnp.logical_not(self.net.middle))
+        def _():
+            for slot in (1, 2, 3):
+                self.arrived(slot).wait_recv()
+
+    def drain(self):
+        @pl.when(self.net.middle)
+        def _():
+            for hop in self.hops:
+                hop.wait_send()
+
+
+def turn(low, tables, sign):
+    swing = tables[1] * pltpu.roll(low, 96, 1) + tables[2] * pltpu.roll(low, 32, 1)
+    return low * tables[0] + sign * swing
+
+
+def gather_kernel(
+    x, og, norms, w_qkv, w_dense, w_fc, w_proj, b_qkv, b_fc, tables,
+    o_proj, o_fc, o_dense, o_h2, o_dy, o_dys, o_g, o_slope, o_attn, o_hat, o_xh,
+    r_proj, r_qkv, r_dense, o_stats, o_vecs, o_bias,
+    g_qkv, g_dense, g_fc, xs, dys_in, pks, stats, rows, h1c, h1s, h2c, h2s, dyc, dys, xh,
+    qb, kb, vb, probs, probs_low, score_low, oc, dob, dqc, gc, slope, hat, stage, r_q, r_d,
+    send_sems, recv_sems, local_sems, stage_sems,
+):
+    tok = x.shape[0]
+    heads = qb.shape[0]
+    scale = 1.0 / math.sqrt(HD)
+    net = Net(send_sems, recv_sems, local_sems)
+    net.barrier()
+    qkv = Gather(net, w_qkv, g_qkv, True)
+    dense = Gather(net, w_dense, g_dense, False)
+    fc = Gather(net, w_fc, g_fc, True)
+    proj = Gather(net, w_proj, o_proj, False)
+    qkv.send_own()
+    dense.send_own()
+
+    step = 128
+    lane = lax.broadcasted_iota(jnp.int32, (step, 128), 1)
+    o_bias[...] = jnp.zeros_like(o_bias)
+
+    def local_norm(n, _):
+        at = span(n * step, step)
+        block = x[at, :]
+        mean = jnp.mean(block, axis=1, keepdims=True)
+        centred = block - mean
+        var = jnp.mean(centred * centred, axis=1, keepdims=True)
+        xs[0, at, :] = (centred * lax.rsqrt(var + epsilon)).astype(bf16)
+        stats[at, :] = jnp.where(lane == 0, mean, jnp.where(lane == 1, var, 0.0))
+        return 0
+
+    lax.fori_loop(0, tok // step, local_norm, 0)
+    pks[0] = stats[...].T[0:8]
+    pks[0, 2:6, :] = norms[...]
+    packs = [net.remote(pks.at[0], pks.at[j], net.z[j]) for j in (1, 2, 3)]
+    x_line = Line(net, xs)
+    x_line.start()
+    for weight in (qkv, dense, fc):
+        weight.place_own()
+
+    def local_grad(n, _):
+        at = span(n * step, step)
+        block = og[at, :]
+        dys_in[0, at, :] = block.astype(bf16)
+        o_bias[1:2, 0:512] += jnp.sum(block, axis=0, keepdims=True)
+        return 0
+
+    lax.fori_loop(0, tok // step, local_grad, 0)
+    qkv.forward()
+    x_line.step(0)
+    x_line.step(1)
+    fc.send_own()
+    dense.forward()
+    qkv.swap_near()
+    x_line.step(2)
+    y_line = Line(net, dys_in)
+    y_line.start()
+    dense.swap_near()
+    qkv.swap_far()
+    dense.swap_far()
+
+    for pack in packs:
+        pack.wait_recv()
+    means = [pks[j, 0:1, :] for j in range(4)]
+    vars_ = [pks[j, 1:2, :] for j in range(4)]
+    mu = (means[0] + means[1] + means[2] + means[3]) * 0.25
+    spread = [vars_[j] + (means[j] - mu) * (means[j] - mu) for j in range(4)]
+    rstd = lax.rsqrt((spread[0] + spread[1] + spread[2] + spread[3]) * 0.25 + epsilon)
+    rows[...] = jnp.zeros_like(rows)
+    for j in range(4):
+        rows[j : j + 1, :] = jnp.sqrt(vars_[j] + epsilon) * rstd
+        rows[4 + j : 5 + j, :] = (means[j] - mu) * rstd
+    rows[8:9, :] = mu
+    rows[9:10, :] = rstd
+    stats[...] = rows[...].T
+    o_stats[...] = stats[...]
+    x_line.ready()
+    for s in range(2):
+        for j in range(4):
+            lanes = span(flip(s, net.k) * Q, Q)
+            dest = span(net.mix(j) * Q, Q)
+            wide = span(s * HALF + net.mix(j) * Q, Q)
+            o_vecs[0:4, wide] = pks[j, 2:6, lanes]
+
+            def norm(n, _, s=s, j=j, lanes=lanes, dest=dest, wide=wide):
+                at = span(n * step, step)
+                hat_x = xs[j, at, lanes].astype(f32) * stats[at, j : j + 1] + stats[at, 4 + j : 5 + j]
+                xh[at, wide] = hat_x.astype(bf16)
+                one = hat_x * pks[j, 2:3, lanes] + pks[j, 3:4, lanes]
+                two = hat_x * pks[j, 4:5, lanes] + pks[j, 5:6, lanes]
+                (h1s if s else h1c)[at, dest] = one.astype(bf16)
+                (h2s if s else h2c)[at, dest] = two.astype(bf16)
+                return 0
+
+            lax.fori_loop(0, tok // step, norm, 0)
+    swaps = [
+        net.remote(h1s, h1c.at[pl.ds(tok, tok), :], net.core),
+        net.remote(h2s, h2c.at[pl.ds(tok, tok), :], net.core),
+    ]
+    mine = pl.ds(0, tok)
+    theirs = pl.ds(tok, tok)
+    fc.forward()
+    y_line.step(0)
+    qkv.ready()
+
+    def project(n, _):
+        cols = span(n * 3 * HD, 3 * HD)
+        acc = mm(h1c[mine, :], g_qkv[0:HALF, cols]) + mm(h1s[...], g_qkv[HALF:, cols])
+        acc = acc + b_qkv[:, cols]
+        qb[n, :, 0:128] = turn(acc[:, 0:128], tables, 1.0).astype(bf16)
+        qb[n, :, 128:HD] = acc[:, 128:HD].astype(bf16)
+        kb[n, :, 0:128] = turn(acc[:, HD : HD + 128], tables, 1.0).astype(bf16)
+        kb[n, :, 128:HD] = acc[:, HD + 128 : 2 * HD].astype(bf16)
+        vb[n] = acc[:, 2 * HD :].astype(bf16)
+        return 0
+
+    lax.fori_loop(0, heads, project, 0)
+    proj.send_own()
+    y_line.step(1)
+
+    chunks = tok // step
+
+    def attend(n, _):
+        head, chunk = n // chunks, n % chunks
+        at = span(chunk * step, step)
+        scores = mm_nt(qb[head, at, :], kb[head]) * scale
+        token = lax.broadcasted_iota(jnp.int32, (step, tok), 0) + chunk * step
+        allowed = token >= lax.broadcasted_iota(jnp.int32, (step, tok), 1)
+        scores = jnp.where(allowed, scores, -1e30)
+        top = jnp.max(scores, axis=1, keepdims=True)
+        raised = jnp.where(allowed, jnp.exp(scores - top), 0.0)
+        weight = raised / jnp.sum(raised, axis=1, keepdims=True)
+        probs[head, at, :] = weight
+        low = weight.astype(bf16)
+        probs_low[head, at, :] = low
+        oc[at, span(head * HD, HD)] = mm(low, vb[head]).astype(bf16)
+        return 0
+
+    lax.fori_loop(0, heads * chunks, attend, 0)
+    swaps.append(net.remote(oc.at[mine, :], oc.at[theirs, :], net.core))
+    outs = [net.local(oc.at[mine, :], o_attn)]
+    fc.swap_near()
+    y_line.step(2)
+    fc.swap_far()
+    fc.ready()
+    outs.append(net.local(g_fc, o_fc))
+
+    def expand(n, _):
+        cols = span(n * 512, 512)
+        a = mm(h2c[mine, :], g_fc[0:HALF, cols]) + mm(h2s[...], g_fc[HALF:, cols])
+        a = a + b_fc[:, cols]
+        rise = 0.5 * (1.0 + lax.erf(a * 0.7071067811865476))
+        gc[mine, cols] = (a * rise).astype(bf16)
+        slope[:, cols] = (rise + a * 0.3989422804014327 * jnp.exp(-0.5 * a * a)).astype(bf16)
+        return 0
+
+    lax.fori_loop(0, gc.shape[1] // 512, expand, 0)
+    swaps.append(net.remote(gc.at[mine, :], gc.at[theirs, :], net.core))
+    outs.append(net.local(gc.at[mine, :], o_g))
+    outs.append(net.local(slope, o_slope))
+    outs.append(net.local(xh, o_xh))
+    proj.forward()
+
+    y_line.ready()
+    for s in range(2):
+        for j in range(4):
+            lanes = span(flip(s, net.k) * Q, Q)
+            dest = span(net.mix(j) * Q, Q)
+            (dys if s else dyc)[mine, dest] = dys_in[j, :, lanes]
+    swaps.append(net.remote(dys, dyc.at[theirs, :], net.core))
+    outs.append(net.local(dyc.at[mine, :], o_dy))
+    outs.append(net.local(dys, o_dys))
+    dense.ready()
+    outs.append(net.local(g_dense, o_dense))
+    dob[...] = (
+        mm_nt(dyc[mine, :], g_dense[:, 0:HALF]) + mm_nt(dys[...], g_dense[:, HALF:])
+    ).astype(bf16)
+
+    def keep(head, part, at, value, rotated):
+        base = head * 3 * HD + part * HD
+        if rotated:
+            low = turn(value[:, 0:128], [tables[t, at, :] for t in range(3)], -1.0)
+            dqc[at, pl.ds(pl.multiple_of(base, 128), 128)] = low.astype(bf16)
+            o_bias[0:1, pl.ds(pl.multiple_of(base, 128), 128)] += jnp.sum(low, axis=0, keepdims=True)
+            value, base, width = value[:, 128:], base + 128, 128
+        else:
+            width = HD
+        cols = pl.ds(pl.multiple_of(base, 128), width)
+        dqc[at, cols] = value.astype(bf16)
+        o_bias[0:1, cols] += jnp.sum(value, axis=0, keepdims=True)
+
+    def attend_back(head, _):
+        cols = span(head * HD, HD)
+
+        def chunk_back(n, _):
+            at = span(n * step, step)
+            grad = dob[at, cols]
+            delta = jnp.sum(grad.astype(f32) * oc[at, cols].astype(f32), axis=1, keepdims=True)
+            spread = mm_nt(grad, vb[head]) - delta
+            low = (probs[head, at, :] * spread * scale).astype(bf16)
+            score_low[at, :] = low
+            keep(head, 0, at, mm(low, kb[head]), True)
+            return 0
+
+        lax.fori_loop(0, chunks, chunk_back, 0)
+        whole = pl.ds(0, tok)
+        keep(head, 1, whole, mm_tn(score_low[...], qb[head]), True)
+        keep(head, 2, whole, mm_tn(probs_low[head], dob[:, cols]), False)
+        return 0
+
+    lax.fori_loop(0, heads, attend_back, 0)
+    swaps.append(net.remote(dqc.at[mine, :], dqc.at[theirs, :], net.core))
+    for copy in swaps:
+        copy.wait_recv()
+    outs.append(net.local(h2c, o_h2))
+    proj.swap_near()
+
+    def grad_proj(n, _):
+        cols = span(n * 512, 512)
+        part = mm_tn(gc[:, cols], dyc[...]).astype(bf16)
+        slot = n % 2
+        copy = pltpu.make_async_copy(stage.at[slot], r_proj.at[cols, :], stage_sems.at[slot])
+
+        @pl.when(n >= 2)
+        def _():
+            copy.wait()
+
+        stage[slot] = part
+        copy.start()
+        return 0
+
+    lax.fori_loop(0, gc.shape[1] // 512, grad_proj, 0)
+    for slot in range(2):
+        pltpu.make_async_copy(stage.at[slot], r_proj.at[0:512, :], stage_sems.at[slot]).wait()
+
+    def grad_qkv(n, _):
+        cols = span(n * 512, 512)
+        r_q[:, cols] = mm_tn(h1c[...], dqc[:, cols]).astype(bf16)
+        return 0
+
+    lax.fori_loop(0, dqc.shape[1] // 512, grad_qkv, 0)
+    outs.append(net.local(r_q, r_qkv))
+    r_d[...] = mm_tn(oc[...], dyc[...]).astype(bf16)
+    outs.append(net.local(r_d, r_dense))
+    proj.swap_far()
+
+    def grad_norm(n, _):
+        cols = span(n * 512, 512)
+        grad = mm_nt(dqc[mine, :], g_qkv[cols, :])
+        hat[:, cols] = (grad * o_vecs[0:1, cols]).astype(bf16)
+        o_vecs[4:5, cols] = jnp.sum(grad * xh[:, cols].astype(f32), axis=0, keepdims=True)
+        o_vecs[5:6, cols] = jnp.sum(grad, axis=0, keepdims=True)
+        return 0
+
+    lax.fori_loop(0, 2 * HALF // 512, grad_norm, 0)
+    o_vecs[6:8, :] = jnp.zeros((2, 2 * HALF), f32)
+    outs.append(net.local(hat, o_hat))
+    proj.ready()
+    for copy in outs:
+        copy.wait()
+    net.drain()
+    x_line.drain()
+    y_line.drain()
+
+
+def call_gather(x, og, norms, w_qkv, w_dense, w_fc, w_proj, b_qkv, b_fc, tables):
+    tok = x.shape[0]
+    n_qkv, n_attn, n_fc = w_qkv.shape[1], w_dense.shape[0], w_fc.shape[1]
+    heads = n_attn // HD
+    wide = 2 * HALF
+    any_spec = pl.BlockSpec(memory_space=pl.ANY)
+    vmem = pl.BlockSpec(memory_space=VMEM)
+    shape = jax.ShapeDtypeStruct
+    outs = [
+        shape((n_fc, wide), bf16), shape((wide, n_fc), bf16), shape((n_attn, wide), bf16),
+        shape((2 * tok, HALF), bf16), shape((tok, HALF), bf16), shape((tok, HALF), bf16),
+        shape((tok, n_fc), bf16), shape((tok, n_fc), bf16), shape((tok, n_attn), bf16),
+        shape((tok, wide), bf16), shape((tok, wide), bf16),
+        shape((n_fc, HALF), bf16), shape((HALF, n_qkv), bf16), shape((n_attn, HALF), bf16),
+        shape((tok, 128), f32), shape((8, wide), f32), shape((8, wide), f32),
+    ]
+    scratch = [
+        VMEM((wide, n_qkv), bf16), VMEM((n_attn, wide), bf16), VMEM((wide, n_fc), bf16),
+        VMEM((4, tok, 512), bf16), VMEM((4, tok, 512), bf16), VMEM((4, 8, tok), f32),
+        VMEM((tok, 128), f32), VMEM((128, tok), f32),
+        VMEM((2 * tok, HALF), bf16), VMEM((tok, HALF), bf16),
+        VMEM((2 * tok, HALF), bf16), VMEM((tok, HALF), bf16),
+        VMEM((2 * tok, HALF), bf16), VMEM((tok, HALF), bf16), VMEM((tok, wide), bf16),
+        VMEM((heads, tok, HD), bf16), VMEM((heads, tok, HD), bf16), VMEM((heads, tok, HD), bf16),
+        VMEM((heads, tok, tok), f32), VMEM((heads, tok, tok), bf16), VMEM((tok, tok), bf16),
+        VMEM((2 * tok, n_attn), bf16), VMEM((tok, n_attn), bf16), VMEM((2 * tok, n_qkv), bf16),
+        VMEM((2 * tok, n_fc), bf16), VMEM((tok, n_fc), bf16), VMEM((tok, wide), bf16),
+        VMEM((2, 512, HALF), bf16), VMEM((HALF, n_qkv), bf16), VMEM((n_attn, HALF), bf16),
+        pltpu.SemaphoreType.DMA((64,)), pltpu.SemaphoreType.DMA((64,)),
+        pltpu.SemaphoreType.DMA((32,)), pltpu.SemaphoreType.DMA((2,)),
+    ]
+    return pl.pallas_call(
+        gather_kernel,
+        name="gather_and_forward",
+        out_shape=outs,
+        in_specs=[vmem] * 3 + [any_spec] * 4 + [vmem] * 3,
+        out_specs=[any_spec] * 14 + [vmem] * 3,
+        scratch_shapes=scratch,
+        compiler_params=pltpu.CompilerParams(
+            collective_id=1, has_side_effects=True, vmem_limit_bytes=67043328
+        ),
+    )(x, og, norms, w_qkv, w_dense, w_fc, w_proj, b_qkv, b_fc, tables)
+
+
+class Reduce:
+    def __init__(self, net, partial, part, joined, near, far, by_rows):
+        self.net, self.partial, self.by_rows = net, partial, by_rows
+        self.part, self.joined, self.near, self.far = part, joined, near, far
+        self.depth = Q // 2 if by_rows else partial.shape[0] // 2
+
+    def chunk(self, i, half):
+        if self.by_rows:
+            return self.partial.at[pl.ds(i * Q + half * self.depth, self.depth), :]
+        return self.partial.at[pl.ds(half * self.depth, self.depth), pl.ds(i * Q, Q)]
+
+    def whole(self):
+        if self.by_rows:
+            return self.partial.at[pl.ds(0, Q), :]
+        return self.partial.at[:, pl.ds(0, Q)]
+
+    def rows(self, half):
+        return pl.ds(half * self.depth, self.depth)
+
+    def start(self):
+        net = self.net
+        self.loads = [
+            net.local(self.chunk(2, 0), self.part.at[0]),
+            net.local(self.chunk(1, 1), self.part.at[1]),
+        ]
+        self.a = net.remote(self.chunk(3, 0), self.joined.at[0], net.x)
+        self.b = net.remote(self.chunk(3, 1), self.joined.at[1], net.y)
+        self.near_a = net.remote(self.chunk(1, 0), self.near.at[self.rows(0), :], net.x)
+        self.near_b = net.remote(self.chunk(2, 1), self.near.at[self.rows(1), :], net.y)
+
+    def join(self):
+        net = self.net
+        hops = []
+        for half, copy, peer in ((0, self.a, net.y), (1, self.b, net.x)):
+            self.loads[half].wait()
+            copy.wait_recv()
+            tile = 64
+
+            def add(n, _, half=half):
+                at = span(n * tile, tile)
+                total = self.joined[half, at, :].astype(f32) + self.part[half, at, :].astype(f32)
+                self.part[half, at, :] = total.astype(bf16)
+                return 0
+
+            lax.fori_loop(0, self.depth // tile, add, 0)
+            hops.append(net.remote(self.part.at[half], self.far.at[self.rows(half), :], peer))
+        self.far_a, self.far_b = hops
+
+    def finish(self, buffers, total, out):
+        net = self.net
+        loads = [net.local(self.whole(), buffers[0])]
+        for copy in (self.near_a, self.near_b):
+            copy.wait_recv()
+        loads.append(net.local(self.near, buffers[1]))
+        for copy in (self.far_a, self.far_b):
+            copy.wait_recv()
+        loads.append(net.local(self.far, buffers[2]))
+        for copy in loads:
+            copy.wait()
+        tile = 64
+
+        def add(n, _):
+            at = span(n * tile, tile)
+            parts = [buffer[at, :].astype(f32) for buffer in buffers]
+            total[at, :] = parts[0] + parts[1] + parts[2]
+            return 0
+
+        lax.fori_loop(0, total.shape[0] // tile, add, 0)
+        if self.by_rows:
+            place = out.at[span(net.k * Q, Q), :]
+        else:
+            place = out.at[:, span(net.k * Q, Q)]
+        return [net.local(total, place)], [net.remote(total, place, net.core)]
+
+
+def reduce_kernel(
+    w_proj, i_proj, i_fc, i_dense, i_h2, i_dy, i_dys, i_g, i_slope, i_attn, i_hat, i_xh,
+    r_proj, r_qkv, r_dense, vecs, bias,
+    o_proj, o_qkv, o_fc, o_dense, n_proj, f_proj, n_qkv, f_qkv, n_fc, f_fc, n_dense, f_dense,
+    o_branch, o_hat, o_stats, o_small,
+    g_proj, g_fc, g_dense, g, slope, attn, hat, xh, dy, dys, h2c, dab,
+    out_send, out_recv, hat_send, hat_recv, p_proj, j_proj, p_qkv, j_qkv, p_fc, j_fc, p_dense, j_dense,
+    part_fc, t_proj, t_qkv, t_fc, t_dense, packs, stats, sums, small,
+    send_sems, recv_sems, local_sems,
+):
+    tok = g.shape[0]
+    net = Net(send_sems, recv_sems, local_sems)
+    net.barrier()
+    proj = Reduce(net, r_proj, p_proj, j_proj, n_proj, f_proj, False)
+    qkv = Reduce(net, r_qkv, p_qkv, j_qkv, n_qkv, f_qkv, True)
+    fc = Reduce(net, part_fc, p_fc, j_fc, n_fc, f_fc, True)
+    dense = Reduce(net, r_dense, p_dense, j_dense, n_dense, f_dense, False)
+    load_g = [net.local(i_g, g), net.local(i_attn, attn), net.local(i_dense, g_dense)]
+    for s, half in ((0, net.k), (1, 1 - net.k)):
+        load_g.append(net.local(w_proj.at[:, span(half * Q, Q)], g_proj.at[:, pl.ds(s * HALF, Q)]))
+        rest = pl.ds(s * HALF + Q, HALF - Q)
+        load_g.append(net.local(i_proj.at[:, rest], g_proj.at[:, rest]))
+    proj.start()
+    load_dy = [net.local(i_dy, dy), net.local(i_dys, dys), net.local(i_slope, slope)]
+    load_fc = [net.local(i_fc, g_fc), net.local(i_hat, hat), net.local(i_xh, xh)]
+    load_h2 = net.local(i_h2, h2c)
+    for copy in load_g:
+        copy.wait()
+
+    def lanes_of(s):
+        return span(flip(s, net.k) * Q, Q)
+
+    def project(j, _):
+        for s in range(2):
+            cols = span(s * HALF + net.mix(j) * Q, Q)
+            out = mm(g[...], g_proj[:, cols]) + mm(attn[...], g_dense[:, cols])
+            out_send[j, :, lanes_of(s)] = out.astype(bf16)
+        return 0
+
+    lax.fori_loop(0, 4, project, 0)
+    out_copies = [net.remote(out_send.at[j], out_recv.at[j - 1], net.z[j]) for j in (1, 2, 3)]
+    for copy in load_dy:
+        copy.wait()
+    mine = pl.ds(0, tok)
+    theirs = pl.ds(tok, tok)
+    sums[...] = jnp.zeros_like(sums)
+
+    def back_fc(n, _):
+        cols = span(n * 512, 512)
+        grad = mm_nt(dy[...], g_proj[cols, 0:HALF]) + mm_nt(dys[...], g_proj[cols, HALF:])
+        grad = grad * slope[:, cols].astype(f32)
+        sums[0:1, cols] = jnp.sum(grad, axis=0, keepdims=True)
+        dab[mine, cols] = grad.astype(bf16)
+        return 0
+
+    lax.fori_loop(0, g.shape[1] // 512, back_fc, 0)
+    swap = net.remote(dab.at[mine, :], dab.at[theirs, :], net.core)
+    proj.join()
+    qkv.start()
+    for copy in load_fc:
+        copy.wait()
+    stats[...] = jnp.zeros_like(stats)
+    lane = lax.broadcasted_iota(jnp.int32, (tok, 128), 1)
+
+    def back_norm(j, _):
+        for s in range(2):
+            lanes = lanes_of(s)
+            cols = span(s * HALF + net.mix(j) * Q, Q)
+            grad = mm_nt(dab[mine, :], g_fc[cols, :])
+            hats = xh[:, cols].astype(f32)
+            packs[j, 2:3, lanes] = vecs[4:5, cols]
+            packs[j, 3:4, lanes] = vecs[5:6, cols]
+            packs[j, 4:5, lanes] = jnp.sum(grad * hats, axis=0, keepdims=True)
+            packs[j, 5:6, lanes] = jnp.sum(grad, axis=0, keepdims=True)
+            joint = hat[:, cols].astype(f32) + grad * vecs[2:3, cols]
+            hat_send[j, :, lanes] = joint.astype(bf16)
+            one = jnp.sum(joint, axis=1, keepdims=True)
+            two = jnp.sum(joint * hats, axis=1, keepdims=True)
+            stats[...] += jnp.where(lane == 0, one, jnp.where(lane == 1, two, 0.0))
+        return 0
+
+    lax.fori_loop(0, 4, back_norm, 0)
+    turned = stats[...].T
+    for j in range(4):
+        packs[j, 0:2, :] = turned[0:2]
+        packs[j, 6:8, :] = jnp.zeros((2, tok), f32)
+    pack_copies = [net.remote(packs.at[j], packs.at[3 + j], net.z[j]) for j in (1, 2, 3)]
+    hat_copies = [net.remote(hat_send.at[j], hat_recv.at[j - 1], net.z[j]) for j in (1, 2, 3)]
+    load_h2.wait()
+    swap.wait_recv()
+
+    def grad_fc(n, _):
+        cols = span(n * 512, 512)
+        part_fc[:, cols] = mm_tn(h2c[...], dab[:, cols]).astype(bf16)
+        return 0
+
+    lax.fori_loop(0, dab.shape[1] // 512, grad_fc, 0)
+    outs = []
+
+    def wide(n, columns):
+        return g_proj.at[pl.ds(n * Q, Q), pl.ds(0, columns)]
+
+    def tall(n, count):
+        return g_proj.at[pl.ds(0, count), pl.ds(n * Q, Q)]
+
+    fc.start()
+    local, remote = proj.finish([tall(n, r_proj.shape[0]) for n in range(3)], t_proj, o_proj)
+    outs += local
+    far = remote
+    qkv.join()
+    dense.start()
+    for copy in pack_copies:
+        copy.wait_recv()
+    total = packs[0] + packs[4] + packs[5] + packs[6]
+    stats[...] = jnp.zeros_like(stats)
+    turned_rows = jnp.concatenate([total, jnp.zeros((120, tok), f32)], axis=0)
+    o_stats[...] = turned_rows.T
+    small[0, 0:4, :] = total[2:6, :]
+    for n in range(3):
+        small[0, 4 + n : 5 + n, :] = bias[0:1, n * 512 : n * 512 + 512]
+    for n in range(4):
+        small[0, 7 + n : 8 + n, :] = sums[0:1, n * 512 : n * 512 + 512]
+    small[0, 11:12, :] = bias[1:2, 0:512]
+    small[0, 12:16, :] = jnp.zeros((4, 512), f32)
+    for hop, peer in enumerate((net.core, net.x, net.y)):
+        net.remote(small.at[hop], small.at[4 + hop], peer).wait_recv()
+        small[hop + 1] = small[hop] + small[4 + hop]
+    o_small[...] = small[3]
+    for copy in out_copies:
+        copy.wait_recv()
+
+    def sum_out(n, _):
+        at = span(n * 64, 64)
+        value = out_send[0, at, :].astype(f32)
+        for j in range(3):
+            value = value + out_recv[j, at, :].astype(f32)
+        o_branch[at, :] = value
+        return 0
+
+    lax.fori_loop(0, tok // 64, sum_out, 0)
+    local, remote = qkv.finish([wide(n, r_qkv.shape[1]) for n in range(3)], t_qkv, o_qkv)
+    outs += local
+    far += remote
+    fc.join()
+    for copy in hat_copies:
+        copy.wait_recv()
+
+    def sum_hat(n, _):
+        at = span(n * 64, 64)
+        value = hat_send[0, at, :].astype(f32)
+        for j in range(3):
+            value = value + hat_recv[j, at, :].astype(f32)
+        o_hat[at, :] = value
+        return 0
+
+    lax.fori_loop(0, tok // 64, sum_hat, 0)
+    dense.join()
+    local, remote = fc.finish([wide(n, part_fc.shape[1]) for n in range(3)], t_fc, o_fc)
+    outs += local
+    far += remote
+    local, remote = dense.finish([tall(n, r_dense.shape[0]) for n in range(3)], t_dense, o_dense)
+    outs += local
+    far += remote
+    for copy in outs:
+        copy.wait()
+    for copy in far:
+        copy.wait_recv()
+    net.drain()
+
+
+def call_reduce(w_proj, gathered, vecs, bias):
+    tok, wide = gathered[9].shape
+    n_fc, n_attn = gathered[0].shape[0], gathered[2].shape[0]
+    n_qkv = gathered[12].shape[1]
+    any_spec = pl.BlockSpec(memory_space=pl.ANY)
+    vmem = pl.BlockSpec(memory_space=VMEM)
+    shape = jax.ShapeDtypeStruct
+    pieces = ((n_fc, Q), (Q, n_qkv), (Q, n_fc), (n_attn, Q))
+    outs = [
+        shape((n_fc, 2 * Q), f32), shape((2 * Q, n_qkv), f32),
+        shape((2 * Q, n_fc), f32), shape((n_attn, 2 * Q), f32),
+    ]
+    outs += [shape(piece, bf16) for piece in pieces for _ in range(2)]
+    outs += [shape((tok, 512), f32), shape((tok, 512), f32), shape((tok, 128), f32)]
+    outs += [shape((16, 512), f32)]
+    scratch = [
+        VMEM((n_fc, wide), bf16), VMEM((wide, n_fc), bf16), VMEM((n_attn, wide), bf16),
+        VMEM((tok, n_fc), bf16), VMEM((tok, n_fc), bf16), VMEM((tok, n_attn), bf16),
+        VMEM((tok, wide), bf16), VMEM((tok, wide), bf16), VMEM((tok, HALF), bf16),
+        VMEM((tok, HALF), bf16), VMEM((2 * tok, HALF), bf16), VMEM((2 * tok, n_fc), bf16),
+        VMEM((4, tok, 512), bf16), VMEM((3, tok, 512), bf16),
+        VMEM((4, tok, 512), bf16), VMEM((3, tok, 512), bf16),
+    ]
+    for rows, cols in pieces:
+        scratch += [VMEM((2, rows // 2, cols), bf16)] * 2
+    scratch += [VMEM((HALF, n_fc), bf16)]
+    scratch += [VMEM(piece, f32) for piece in pieces]
+    scratch += [
+        VMEM((7, 8, tok), f32), VMEM((tok, 128), f32), VMEM((8, n_fc), f32), VMEM((7, 16, 512), f32),
+        pltpu.SemaphoreType.DMA((48,)), pltpu.SemaphoreType.DMA((48,)), pltpu.SemaphoreType.DMA((48,)),
+    ]
+    return pl.pallas_call(
+        reduce_kernel,
+        name="backward_and_reduce",
+        out_shape=outs,
+        in_specs=[any_spec] * 15 + [vmem] * 2,
+        out_specs=[any_spec] * 12 + [vmem] * 4,
+        scratch_shapes=scratch,
+        compiler_params=pltpu.CompilerParams(
+            collective_id=2, has_side_effects=True, vmem_limit_bytes=67043328
+        ),
+    )(w_proj, *gathered, vecs, bias)
+
+
+def turn_tables(length):
+    half_rot = ROT // 2
+    frequency = (10000.0 ** (-np.arange(half_rot, dtype=np.float32) * (2.0 / ROT))).astype(np.float32)
+    angles = np.arange(length, dtype=np.float32)[:, None] * frequency[None, :]
+    tables = np.zeros((3, length, 128), np.float32)
+    tables[0] = 1.0
+    tables[0, :, :half_rot] = tables[0, :, half_rot:ROT] = np.cos(angles)
+    tables[1, :, :half_rot] = -np.sin(angles)
+    tables[2, :, half_rot:ROT] = np.sin(angles)
+    return tables
+
+
+def fused_shards(
+    block_input, out_grad, ln1_gain, ln1_bias, ln2_gain, ln2_bias,
+    w_qkv, b_qkv, w_dense, b_dense, w_fc, b_fc, w_proj, b_proj,
+):
+    norms = jnp.stack([ln1_gain, ln1_bias, ln2_gain, ln2_bias])
+    *gathered, stats, vecs, bias = call_gather(
+        block_input, out_grad, norms, w_qkv, w_dense, w_fc, w_proj,
+        b_qkv[None, :], b_fc[None, :], turn_tables(SEQ),
+    )
+    reduced = call_reduce(w_proj, gathered, vecs, bias)
+    proj_total, qkv_total, fc_total, dense_total = reduced[:4]
+    branch, hat_grad, totals, small = reduced[12:]
+    block_output = block_input + branch + (b_dense + b_proj)
+    x_hat = (block_input - stats[:, 8:9]) * stats[:, 9:10]
+    input_grad = out_grad + stats[:, 9:10] * (
+        hat_grad - totals[:, 0:1] * (1.0 / D) - x_hat * (totals[:, 1:2] * (1.0 / D))
+    )
+    return (
+        block_output, input_grad, small[0], small[1], small[2], small[3],
+        qkv_total, small[4:7].reshape(-1), dense_total, small[11],
+        fc_total, small[7:11].reshape(-1), proj_total, small[11],
+    )
+
+
 def solution(mesh):
+    sizes = tuple(mesh.shape[name] for name in ("dp", "row", "col"))
+    body = fused_shards if sizes == (2, 4, 4) else shards
     return jax.shard_map(
-        shards,
+        body,
         mesh=mesh,
         in_specs=(
             P(("dp", "row"), "col"),

time: 1310 us -> 268 us (0.20)
  waiting for transfers between devices: 1040 us -> 0 us
  Pallas kernels: 0 us -> 246 us
  matrix products: 91.8 us -> 0 us
  other arithmetic: 65.9 us -> 7.8 us
  blocking collectives: 50.8 us -> 0 us
  local copies, waits for them, and re-layouts: 44.2 us -> 13.4 us
  between operations: 14.9 us -> 0.68 us
    reduce_scatter x3 -> x0, waiting for transfers between devices: 577 us -> none  [the longest x1 395 us: shards(): lax.psum_scatter(jnp.concatenate([lax.dot_general(part_one, qkv_grad_low,...]
    all_gather x7 -> x0, waiting for transfers between devices: 407 us -> none  [the longest x1 106 us: shards(): shard_piece = lax.all_gather(out_stack, 'row', axis=1, tiled=True)]
    pallas_call x0 -> x2, Pallas kernels: none -> 246 us  [the longest x1 125 us: call_gather(): pl.pallas_call(gather_kernel, name='gather_and_forward', out_shape=outs,...]
    dot_general x17 -> x0, matrix products: 91.8 us -> none  [the longest x1 9.89 us: shards(): jnp.dot(part_two, lax.all_gather(w_fc, 'row', axis=0, tiled=True), prefer...]
    psum x1 -> x0, waiting for transfers between devices: 50.9 us -> none  [shards(): grad_rows = lax.psum(row_part, 'dp')]
    psum x3 -> x0, blocking collectives: 50.8 us -> none  [the longest x1 28.6 us: shards(): lax.psum((jnp.sum(grad_one * x_hat, axis=0), jnp.sum(grad_one, axis=0), j...]
    concatenate x3 -> x0, other arithmetic: 39.8 us -> none  [the longest x1 32.8 us: shards(): jnp.concatenate([lax.dot_general(part_one, qkv_grad_low, contract_first,...]
  transfers between devices with their start and end apart: 11 -> 0, of which waited for: 11 -> 0; matrix products, arithmetic and copies ran while one was open for 13% -> 0% of each run, Pallas kernels for 0% -> 0%
where the time goes in v1:
time: 268 us; the launch traced here: 267 us
  Pallas kernels  246 us (92%)
  local copies, waits for them, and re-layouts  13.4 us (5%)
  other arithmetic  7.8 us (3%)
    pallas_call x1, Pallas kernels, call_gather(): pl.pallas_call(gather_kernel, name='gather_and_forward', out_shape=outs,...  125 us
    pallas_call x1, Pallas kernels, call_reduce(): pl.pallas_call(reduce_kernel, name='backward_and_reduce', out_shape=outs,...  121 us
    unnamed x19, local copies, waits for them, and re-layouts  10.9 us

profile of v1, /device:TPU:1, one launch (start us, length us, event | category | flops | bytes accessed | tf_op | source)
XLA Modules:
  0.0 267.5 jit_solution(11220280975860550299)
XLA Ops:
  0.6 1.3 pad_maximum_fusion.norms
  2.0 1.3 broadcast_in_dim.7.b_qkv
  3.3 124.6 %gather_and_forward.1 = (bf16[2048,2048]{1,0:T(8,128)(2,1)}, bf16[2048,2048]{1,0:T(8,128)(2,1)}, bf16[512,2048]{1,0:T(8,128)(2,1)}, bf16[1024,1024]{1,0:T(8,128)...) custom-call(f32[512,512]{1,0:T(8,128)} %x.1, ...), custom_call_target="tpu_custom_call" | custom-call | tf_op jit(solution)/shard_map/gather_and_forward/pallas_call | solution.py:811
  127.9 121.0 %backward_and_reduce.1 = (f32[2048,512]{1,0:T(8,128)}, f32[512,1536]{1,0:T(8,128)}, f32[512,2048]{1,0:T(8,128)}, f32[512,512]{1,0:T(8,128)}, bf16[2048,256]{1,0:...) custom-call(bf16[2048,512]{1,0:T(8,128)(2,1)} %w_proj.3, ...), custom_call_target="tpu_custom_call" | custom-call | tf_op jit(solution)/shard_map/backward_and_reduce/pallas_call | solution.py:1100
  248.8 1.8 multiply_reduce_fusion.1
  250.6 0.7 add.18
  251.3 0.0 copy-start.4
  251.3 0.0 copy-start.2
  251.3 4.0 %multiply_add_fusion = (f32[512,512]{1,0:T(8,128)}, f32[512,512]{1,0:T(8,128)}) fusion(f32[512,512]{1,0:T(8,128)} %og.1, f32[512,512]{1,0:T(8,128)} %x.1, f32[512,512]{1,0:T(8,128)} %get-tuple-element.57, f32[512]{0:T(512)S(1)} %get-tuple-element.67, f32[512]{0:T(512)S(1)} %get-tuple-element.75, f32[512]{0:T(512)S(1)} %get-tuple-element.66, ...), kind=kLoop, calls=%fused_computation | loop fusion | flops 2359296 | bytes 6301696 | tf_op jit(solution)/shard_map/add | solution.py:1139
  255.3 0.0 copy-done.4
  255.3 0.6 copy.29
  255.9 0.6 reshape.35
  256.5 0.6 fusion
  257.1 0.0 copy-start.5
  257.1 0.6 copy.35
  257.7 0.0 copy-done.2
  257.7 0.0 copy-start.3
  257.7 0.0 copy-start.1
  257.7 1.7 copy.36
  259.4 0.0 copy-done.5
  259.4 0.3 copy-done.3
  259.7 1.0 copy.37
  260.6 1.1 copy-done.1
  261.7 0.0 copy-start
  261.7 2.1 copy.38
  263.9 1.6 copy-done
  265.4 2.0 copy.39
  (2 shorter events, 0.0 us)
Async XLA Ops:
  251.3 4.0 %copy-start.4 = (f32[16,512]{1,0:T(8,128)S(1)}, f32[16,512]{1,0:T(8,128)}, u32[]{:S(2)}) copy-start(f32[16,512]{1,0:T(8,128)} %get-tuple-element.59) | copy-start | bytes 98308
  251.3 6.4 %copy-start.2 = (f32[512,1536]{1,0:T(8,128)S(1)}, f32[512,1536]{1,0:T(8,128)}, u32[]{:S(2)}) copy-start(f32[512,1536]{1,0:T(8,128)} %get-tuple-element.125) | copy-start | bytes 9437188
  257.1 2.3 copy-start.5
  257.7 2.0 copy-start.3
  257.7 4.0 %copy-start.1 = (f32[512,2048]{1,0:T(8,128)S(1)}, f32[512,2048]{1,0:T(8,128)}, u32[]{:S(2)}) copy-start(f32[512,2048]{1,0:T(8,128)} %get-tuple-element.129) | copy-start | bytes 12582916
  261.7 3.7 %copy-start = (f32[2048,512]{1,0:T(8,128)S(1)}, f32[2048,512]{1,0:T(8,128)}, u32[]{:S(2)}) copy-start(f32[2048,512]{1,0:T(8,128)} %get-tuple-element.131) | copy-start | bytes 12582916

commit v2 on v1

v2 whole, which is shorter than its diff:
```python
import functools
import math

import jax
import jax.numpy as jnp
import numpy as np
from jax import lax
from jax.experimental import pallas as pl
from jax.experimental.pallas import tpu as pltpu
from jax.sharding import PartitionSpec as P

D = 2048
HD = 256
ROT = 64
SEQ = 512


epsilon = 1e-05
contract_last = (((1,), (1,)), ((), ()))
contract_first = (((0,), (0,)), ((), ()))


def angle_tables(length):
    half_rot = ROT // 2
    position = jnp.arange(length, dtype=jnp.float32)
    exponent = jnp.arange(half_rot, dtype=jnp.float32) * (2.0 / ROT)
    frequency = 10000.0 ** (-exponent)
    angles = position[:, None] * frequency[None, :]
    return (jnp.cos(angles), jnp.sin(angles))


def rotate_fwd(values, cosine, sine_vals):
    half_rot = ROT // 2
    first = values[..., :half_rot]
    second = values[..., half_rot:ROT]
    cos_part = cosine[:, None, :]
    sin_part = sine_vals[:, None, :]
    return jnp.concatenate(
        [
            first * cos_part - second * sin_part,
            second * cos_part + first * sin_part,
            values[..., ROT:],
        ],
        axis=-1,
    )


def rotate_back(grads, cosine, sine_vals):
    half_rot = ROT // 2
    first = grads[..., :half_rot]
    second = grads[..., half_rot:ROT]
    cos_part = cosine[:, None, :]
    sin_part = sine_vals[:, None, :]
    return jnp.concatenate(
        [
            first * cos_part + second * sin_part,
            second * cos_part - first * sin_part,
            grads[..., ROT:],
        ],
        axis=-1,
    )


def gelu_value(pre_act):
    return 0.5 * pre_act * (1.0 + lax.erf(pre_act * 0.7071067811865476))


def gelu_slope(pre_act):
    return 0.5 * (
        1.0 + lax.erf(pre_act * 0.7071067811865476)
    ) + pre_act * 0.3989422804014327 * jnp.exp(-0.5 * pre_act * pre_act)


def shards(
    block_input,
    out_grad,
    ln1_gain,
    ln1_bias,
    ln2_gain,
    ln2_bias,
    w_qkv,
    b_qkv,
    w_dense,
    b_dense,
    w_fc,
    b_fc,
    w_proj,
    b_proj,
):
    tok_rows = block_input.shape[0]
    seq_count = tok_rows // SEQ
    qkv_cols = w_qkv.shape[1]
    fc_cols = w_fc.shape[1]
    local_heads = qkv_cols // (3 * HD)
    head_cols = local_heads * HD
    scale = 1.0 / math.sqrt(HD)
    cosine, sine_vals = angle_tables(SEQ)
    causal = jnp.arange(SEQ)[:, None] >= jnp.arange(SEQ)[None, :]
    row_total, square_total = lax.psum(
        (jnp.sum(block_input, axis=1), jnp.sum(block_input * block_input, axis=1)), "col"
    )
    mean_row = (row_total / D)[:, None]
    var_row = (square_total / D)[:, None] - mean_row * mean_row
    inv_std = lax.rsqrt(var_row + epsilon)
    x_hat = (block_input - mean_row) * inv_std
    normed_one = (x_hat * ln1_gain + ln1_bias).astype(jnp.bfloat16)
    normed_two = (x_hat * ln2_gain + ln2_bias).astype(jnp.bfloat16)
    wide_one, wide_two = (
        lax.all_gather(normed_one, "col", axis=1, tiled=True),
        lax.all_gather(normed_two, "col", axis=1, tiled=True),
    )
    part_one = wide_one
    part_two = wide_two
    qkv_pre = jnp.dot(
        part_one,
        lax.all_gather(w_qkv, "row", axis=0, tiled=True),
        preferred_element_type=jnp.float32,
    )
    fc_pre = jnp.dot(
        part_two,
        lax.all_gather(w_fc, "row", axis=0, tiled=True),
        preferred_element_type=jnp.float32,
    )
    qkv_pre = qkv_pre + b_qkv
    fc_pre = fc_pre + b_fc

    def forward_seq(block):
        query = rotate_fwd(block[:, :, 0], cosine, sine_vals).astype(jnp.bfloat16)
        keys = rotate_fwd(block[:, :, 1], cosine, sine_vals).astype(jnp.bfloat16)
        values = block[:, :, 2].astype(jnp.bfloat16)
        scores = jnp.einsum("qhd,khd->hqk", query, keys, preferred_element_type=jnp.float32) * scale
        masked = jnp.where(causal[None], scores, -1e30)
        row_max = jnp.max(masked, axis=-1, keepdims=True)
        exp_sum = jnp.sum(
            jnp.where(causal[None], jnp.exp(masked - row_max), 0.0), axis=-1, keepdims=True
        )
        log_total = row_max + jnp.log(exp_sum)
        probs_low = jnp.where(causal[None], jnp.exp(masked - log_total), 0.0).astype(jnp.bfloat16)
        attended = jnp.einsum(
            "hqk,khd->qhd", probs_low, values, preferred_element_type=jnp.float32
        ).astype(jnp.bfloat16)
        return (query, keys, values, attended, log_total)

    query, keys, values, attended, log_total = lax.map(
        forward_seq, qkv_pre.reshape(seq_count, SEQ, local_heads, 3, HD)
    )
    attn_out = attended.reshape(tok_rows, head_cols)
    gelu_out = gelu_value(fc_pre).astype(jnp.bfloat16)
    out_stack = jnp.concatenate([w_dense, w_proj], axis=0)
    shard_piece = lax.all_gather(out_stack, "row", axis=1, tiled=True)
    mixed = jnp.dot(
        attn_out, shard_piece[:head_cols], preferred_element_type=jnp.float32
    ) + jnp.dot(gelu_out, shard_piece[head_cols:], preferred_element_type=jnp.float32)
    branch_sum = lax.psum_scatter(mixed, "col", scatter_dimension=1, tiled=True)
    block_output = block_input + branch_sum + b_dense + b_proj
    grad_low = out_grad.astype(jnp.bfloat16)
    wide_grad = lax.all_gather(grad_low, "col", axis=1, tiled=True)
    both_grad = lax.dot_general(
        wide_grad,
        lax.all_gather(out_stack, "row", axis=1, tiled=True),
        contract_last,
        preferred_element_type=jnp.float32,
    )
    attn_grad = both_grad[:, :head_cols]
    gelu_grad = both_grad[:, head_cols:]
    attn_grad_low = attn_grad.astype(jnp.bfloat16)
    fc_grad = gelu_grad * gelu_slope(fc_pre)
    fc_bias_grad = jnp.sum(fc_grad, axis=0)
    fc_grad_low = fc_grad.astype(jnp.bfloat16)

    def backward_seq(items):
        query_s, keys_s, values_s, attended_s, log_s, head_grad = items
        scores = (
            jnp.einsum("qhd,khd->hqk", query_s, keys_s, preferred_element_type=jnp.float32) * scale
        )
        probs = jnp.where(
            causal[None], jnp.exp(jnp.where(causal[None], scores, -1e30) - log_s), 0.0
        )
        probs_low = probs.astype(jnp.bfloat16)
        value_grad = jnp.einsum(
            "hqk,qhd->khd", probs_low, head_grad, preferred_element_type=jnp.float32
        )
        prob_grad = jnp.einsum(
            "qhd,khd->hqk", head_grad, values_s, preferred_element_type=jnp.float32
        )
        delta_row = jnp.transpose(
            jnp.sum(head_grad.astype(jnp.float32) * attended_s.astype(jnp.float32), axis=-1), (1, 0)
        )[:, :, None]
        score_grad = (probs * (prob_grad - delta_row) * scale).astype(jnp.bfloat16)
        query_grad = jnp.einsum(
            "hqk,khd->qhd", score_grad, keys_s, preferred_element_type=jnp.float32
        )
        key_grad = jnp.einsum(
            "hqk,qhd->khd", score_grad, query_s, preferred_element_type=jnp.float32
        )
        return jnp.stack(
            [
                rotate_back(query_grad, cosine, sine_vals),
                rotate_back(key_grad, cosine, sine_vals),
                value_grad,
            ],
            axis=2,
        )

    head_grads = attn_grad_low.reshape(seq_count, SEQ, local_heads, HD)
    qkv_grad = lax.map(
        backward_seq, (query, keys, values, attended, log_total, head_grads)
    ).reshape(tok_rows, qkv_cols)
    qkv_bias_grad = jnp.sum(qkv_grad, axis=0)
    qkv_grad_low = qkv_grad.astype(jnp.bfloat16)
    in_stack = jnp.concatenate([w_qkv, w_fc], axis=1)
    shard_piece = lax.all_gather(in_stack, "row", axis=0, tiled=True)
    norm_grads = jnp.stack(
        [
            lax.dot_general(
                qkv_grad_low,
                shard_piece[:, :qkv_cols],
                contract_last,
                preferred_element_type=jnp.float32,
            ),
            lax.dot_general(
                fc_grad_low,
                shard_piece[:, qkv_cols:],
                contract_last,
                preferred_element_type=jnp.float32,
            ),
        ]
    )
    part_one = wide_one
    part_two = wide_two
    row_part = lax.psum_scatter(
        jnp.concatenate(
            [
                lax.dot_general(
                    part_one, qkv_grad_low, contract_first, preferred_element_type=jnp.float32
                ),
                lax.dot_general(
                    part_two, fc_grad_low, contract_first, preferred_element_type=jnp.float32
                ),
                lax.dot_general(
                    wide_grad, attn_out, contract_first, preferred_element_type=jnp.float32
                ),
                lax.dot_general(
                    wide_grad, gelu_out, contract_first, preferred_element_type=jnp.float32
                ),
            ],
            axis=1,
        ),
        "row",
        scatter_dimension=0,
        tiled=True,
    )
    grad_rows = lax.psum(row_part, "dp")
    qkv_total = grad_rows[:, :qkv_cols]
    fc_total = grad_rows[:, qkv_cols : qkv_cols + fc_cols]
    dense_total = grad_rows[:, qkv_cols + fc_cols : qkv_cols + fc_cols + head_cols].T
    proj_total = grad_rows[:, qkv_cols + fc_cols + head_cols :].T
    norm_local = lax.psum_scatter(norm_grads, "col", scatter_dimension=2, tiled=True)
    grad_one = norm_local[0]
    grad_two = norm_local[1]
    hat_grad = grad_one * ln1_gain + grad_two * ln2_gain
    total_hat, total_cross = lax.psum(
        (jnp.sum(hat_grad, axis=1), jnp.sum(hat_grad * x_hat, axis=1)), "col"
    )
    input_grad = out_grad + inv_std * (
        hat_grad - (total_hat / D)[:, None] - x_hat * (total_cross / D)[:, None]
    )
    gain_one, shift_one, gain_two, shift_two, qkv_bias_total, fc_bias_total, out_bias_total = (
        lax.psum(
            (
                jnp.sum(grad_one * x_hat, axis=0),
                jnp.sum(grad_one, axis=0),
                jnp.sum(grad_two * x_hat, axis=0),
                jnp.sum(grad_two, axis=0),
                qkv_bias_grad,
                fc_bias_grad,
                jnp.sum(out_grad, axis=0),
            ),
            ("dp", "row"),
        )
    )
    return (
        block_output,
        input_grad,
        gain_one,
        shift_one,
        gain_two,
        shift_two,
        qkv_total,
        qkv_bias_total,
        dense_total,
        out_bias_total,
        fc_total,
        fc_bias_total,
        proj_total,
        out_bias_total,
    )


f32 = jnp.float32
bf16 = jnp.bfloat16
MESH = pl.DeviceIdType.MESH
VMEM = pltpu.VMEM
Q = 256
HALF = 4 * Q


def flip(a, b):
    return a + b - 2 * a * b


def span(start, size):
    return pl.ds(pl.multiple_of(start, size), size)


def mm(a, b):
    return jnp.dot(a, b, preferred_element_type=f32)


def mm_nt(a, b):
    return lax.dot_general(a, b, (((1,), (1,)), ((), ())), preferred_element_type=f32)


def mm_tn(a, b):
    return lax.dot_general(a, b, (((0,), (0,)), ((), ())), preferred_element_type=f32)


class Net:
    def __init__(self, send_sems, recv_sems, local_sems):
        self.k = lax.axis_index("dp")
        self.r = lax.axis_index("row")
        self.c = lax.axis_index("col")
        k, r, c = self.k, self.r, self.c
        self.core = (1 - k, r, c)
        self.x = (k, r + 1 - 2 * (r % 2), c)
        self.y = (k, r + 2 - 4 * (r // 2), c)
        near = c + 1 - 2 * (c % 2)
        self.z = (None, (k, r, near), (k, r, c + 2 - 4 * (c // 2)), (k, r, 3 - c))
        self.middle = flip(c % 2, c // 2) == 1
        self.send_sems, self.recv_sems, self.local_sems = send_sems, recv_sems, local_sems
        self.remote_count = 0
        self.local_count = 0
        self.pending = []

    def mix(self, j):
        return flip(j % 2, flip(self.c % 2, self.r % 2)) + 2 * flip(
            j // 2, flip(self.c // 2, self.r // 2)
        )

    def barrier(self):
        sem = pltpu.get_barrier_semaphore()
        peers = (self.core, self.x, self.y) + self.z[1:]
        for peer in peers:
            pl.semaphore_signal(sem, inc=1, device_id=peer, device_id_type=MESH)
        pl.semaphore_wait(sem, len(peers))

    def slot(self):
        self.remote_count += 1
        return self.remote_count - 1

    def remote(self, src, dst, peer):
        slot = self.slot()
        copy = pltpu.make_async_remote_copy(
            src_ref=src,
            dst_ref=dst,
            send_sem=self.send_sems.at[slot],
            recv_sem=self.recv_sems.at[slot],
            device_id=peer,
            device_id_type=MESH,
        )
        copy.start()
        self.pending.append(copy)
        return copy

    def local(self, src, dst):
        copy = pltpu.make_async_copy(src, dst, self.local_sems.at[self.local_count])
        self.local_count += 1
        copy.start()
        return copy

    def sent(self, copy):
        copy.wait_send()
        self.pending = [other for other in self.pending if other is not copy]

    def drain(self):
        for copy in self.pending:
            copy.wait_send()


class Gather:
    def __init__(self, net, shard, full, by_rows):
        self.net, self.shard, self.full, self.by_rows = net, shard, full, by_rows
        self.depth = Q // 2 if by_rows else shard.shape[0] // 2
        self.placed = []

    def own(self, half, part=None):
        if self.by_rows:
            if part is None:
                return self.shard.at[span(half * Q, Q), :]
            return self.shard.at[span(half * Q + part * self.depth, self.depth), :]
        rows = slice(None) if part is None else pl.ds(part * self.depth, self.depth)
        return self.shard.at[rows, span(half * Q, Q)]

    def chunk(self, s, i, part=None):
        start = s * HALF + i * Q
        if self.by_rows:
            if part is None:
                return self.full.at[pl.ds(start, Q), :]
            return self.full.at[pl.ds(start + part * self.depth, self.depth), :]
        rows = slice(None) if part is None else pl.ds(part * self.depth, self.depth)
        return self.full.at[rows, pl.ds(start, Q)]

    def place_own(self):
        net = self.net
        self.placed = [
            net.local(self.own(net.k), self.chunk(0, 0)),
            net.local(self.own(1 - net.k), self.chunk(1, 0)),
        ]

    def send_own(self):
        net, k = self.net, self.net.k
        self.y0 = net.remote(self.own(k, 0), self.chunk(0, 2, 0), net.y)
        self.x1 = net.remote(self.own(k, 1), self.chunk(0, 1, 1), net.x)
        self.y1 = net.remote(self.own(k, 1), self.chunk(0, 2, 1), net.y)
        self.x0 = net.remote(self.own(k, 0), self.chunk(0, 1, 0), net.x)

    def forward(self):
        net = self.net
        self.y0.wait_recv()
        self.d0 = net.remote(self.chunk(0, 2, 0), self.chunk(0, 3, 0), net.x)
        self.x1.wait_recv()
        self.d1 = net.remote(self.chunk(0, 1, 1), self.chunk(0, 3, 1), net.y)

    def swap_near(self):
        net = self.net
        self.x0.wait_recv()
        self.c1 = net.remote(self.chunk(0, 1), self.chunk(1, 1), net.core)
        self.y1.wait_recv()
        self.c2 = net.remote(self.chunk(0, 2), self.chunk(1, 2), net.core)

    def swap_far(self):
        net = self.net
        self.d0.wait_recv()
        self.d1.wait_recv()
        self.c3 = net.remote(self.chunk(0, 3), self.chunk(1, 3), net.core)

    def ready(self):
        for copy in (self.c1, self.c2, self.c3):
            copy.wait_recv()
        for copy in self.placed:
            copy.wait()

    def release(self):
        for copy in (self.d0, self.d1, self.c1, self.c2, self.c3):
            self.net.sent(copy)


class Line:
    def __init__(self, net, slots):
        self.net, self.slots = net, slots
        self.ids = [None] + [net.slot() for _ in range(3)]
        self.sends = []

    def copy(self, src, dst, peer, send):
        net = self.net
        return pltpu.make_async_remote_copy(
            src_ref=self.slots.at[src],
            dst_ref=self.slots.at[dst],
            send_sem=net.send_sems.at[send],
            recv_sem=net.recv_sems.at[self.ids[dst]],
            device_id=peer,
            device_id_type=MESH,
        )

    def start(self):
        net = self.net
        self.first = self.copy(0, 1, net.z[1], self.ids[1])
        self.first.start()
        self.hops = [
            self.copy(0, 3, net.z[3], self.ids[2]),
            self.copy(1, 2, net.z[3], self.ids[3]),
            self.copy(3, 2, net.z[1], net.slot()),
            self.copy(2, 3, net.z[1], net.slot()),
        ]

        @pl.when(net.middle)
        def _():
            self.hops[0].start()

    def arrived(self, slot):
        return self.copy(0, slot, self.net.z[1], self.ids[slot])

    def step(self, number):
        slot = (1, 3, 2)[number]

        @pl.when(self.net.middle)
        def _():
            self.arrived(slot).wait_recv()
            self.hops[number + 1].start()

    def ready(self):
        @pl.when(jnp.logical_not(self.net.middle))
        def _():
            for slot in (1, 2, 3):
                self.arrived(slot).wait_recv()

    def drain(self):
        self.first.wait_send()

        @pl.when(self.net.middle)
        def _():
            for hop in self.hops:
                hop.wait_send()


def turn(low, tables, sign):
    swing = tables[1] * pltpu.roll(low, 96, 1) + tables[2] * pltpu.roll(low, 32, 1)
    return low * tables[0] + sign * swing


class Tiles:
    def __init__(self, slots, sems):
        self.slots, self.sems = slots, sems

    def write(self, count, product, place, depth):
        def body(n, _):
            slot = n % 2
            source = self.slots.at[slot, pl.ds(0, depth), :]
            copy = pltpu.make_async_copy(source, place(n), self.sems.at[slot])

            @pl.when(n >= 2)
            def _():
                copy.wait()

            self.slots[slot, 0:depth, :] = product(n).astype(bf16)
            copy.start()
            return 0

        lax.fori_loop(0, count, body, 0)
        for slot in range(2):
            source = self.slots.at[slot, pl.ds(0, depth), :]
            pltpu.make_async_copy(source, place(slot), self.sems.at[slot]).wait()


class Reduce:
    def __init__(self, net, partial, joined, near, far, by_rows):
        self.net, self.partial, self.by_rows = net, partial, by_rows
        self.joined, self.near, self.far = joined, near, far
        self.depth = Q // 2 if by_rows else partial.shape[0] // 2

    def chunk(self, i, half):
        if self.by_rows:
            return self.partial.at[pl.ds(i * Q + half * self.depth, self.depth), :]
        return self.partial.at[pl.ds(half * self.depth, self.depth), pl.ds(i * Q, Q)]

    def whole(self):
        if self.by_rows:
            return self.partial.at[pl.ds(0, Q), :]
        return self.partial.at[:, pl.ds(0, Q)]

    def rows(self, half):
        return pl.ds(half * self.depth, self.depth)

    def start(self):
        net = self.net
        self.a = net.remote(self.chunk(3, 0), self.joined.at[0], net.x)
        self.b = net.remote(self.chunk(3, 1), self.joined.at[1], net.y)
        self.near_a = net.remote(self.chunk(1, 0), self.near.at[self.rows(0), :], net.x)
        self.near_b = net.remote(self.chunk(2, 1), self.near.at[self.rows(1), :], net.y)

    def join(self, parts):
        net = self.net
        loads = [net.local(self.chunk(2, 0), parts[0]), net.local(self.chunk(1, 1), parts[1])]
        hops = []
        for half, copy, peer in ((0, self.a, net.y), (1, self.b, net.x)):
            loads[half].wait()
            copy.wait_recv()
            tile = 64

            def add(n, _, half=half):
                at = span(n * tile, tile)
                total = self.joined[half, at, :].astype(f32) + parts[half][at, :].astype(f32)
                self.joined[half, at, :] = total.astype(bf16)
                return 0

            lax.fori_loop(0, self.depth // tile, add, 0)
            hops.append(net.remote(self.joined.at[half], self.far.at[self.rows(half), :], peer))
        self.far_a, self.far_b = hops

    def finish(self, buffers, out):
        net = self.net
        loads = [net.local(self.whole(), buffers[0])]
        for copy in (self.near_a, self.near_b):
            copy.wait_recv()
        loads.append(net.local(self.near, buffers[1]))
        for copy in (self.far_a, self.far_b):
            copy.wait_recv()
        loads.append(net.local(self.far, buffers[2]))
        for copy in loads:
            copy.wait()
        tile = 64

        def add(n, _):
            at = span(n * tile, tile)
            parts = [buffer[at, :].astype(f32) for buffer in buffers[:3]]
            buffers[3][at, :] = (parts[0] + parts[1] + parts[2]).astype(bf16)
            return 0

        lax.fori_loop(0, self.near.shape[0] // tile, add, 0)
        if self.by_rows:
            place = out.at[span(net.k * Q, Q), :]
        else:
            place = out.at[:, span(net.k * Q, Q)]
        self.here = net.local(buffers[3], place)
        self.there = net.remote(buffers[3], place, net.core)

    def done(self):
        self.here.wait()
        self.there.wait_recv()


def block_kernel(
    x, og, gain_1, bias_1, gain_2, bias_2, w_qkv, w_dense, w_fc, w_proj, b_qkv, b_fc, tables,
    o_proj, o_qkv, o_fc, o_dense, o_branch, o_hat,
    all_proj, r_proj, r_qkv, r_fc, r_dense,
    n_proj, f_proj, n_qkv, f_qkv, n_fc, f_fc, n_dense, f_dense,
    o_stats, o_small,
    g_qkv, g_dense, g_fc, g_tail, xs, ys, pks, stats, rows, h1c, h1s, h2c, h2s, dyc, dys, xh,
    qb, kb, vb, probs, probs_low, score_low, oc, dob, dqc, gc, slope, dabt, stage,
    out_recv, hat_recv, j_proj, j_qkv, j_fc, j_dense, vecs, bias, packs, small,
    send_sems, recv_sems, local_sems, stage_sems,
):
    tok = x.shape[0]
    heads = qb.shape[0]
    width = gc.shape[1]
    scale = 1.0 / math.sqrt(HD)
    net = Net(send_sems, recv_sems, local_sems)
    net.barrier()
    qkv = Gather(net, w_qkv, g_qkv, True)
    dense = Gather(net, w_dense, g_dense, False)
    fc = Gather(net, w_fc, g_fc, True)
    proj = Gather(net, w_proj, all_proj, False)
    qkv.send_own()
    dense.send_own()
    load_x = net.local(x, probs.at[0])
    load_og = net.local(og, probs.at[1])
    tiles = Tiles(stage, stage_sems)
    mine = pl.ds(0, tok)
    theirs = pl.ds(tok, tok)

    step = 128
    lane = lax.broadcasted_iota(jnp.int32, (step, 128), 1)
    load_x.wait()

    def local_norm(n, _):
        at = span(n * step, step)
        block = probs[0, at, :]
        mean = jnp.mean(block, axis=1, keepdims=True)
        centred = block - mean
        var = jnp.mean(centred * centred, axis=1, keepdims=True)
        stats[at, :] = jnp.where(lane == 0, mean, jnp.where(lane == 1, var, 0.0))
        return 0

    lax.fori_loop(0, tok // step, local_norm, 0)
    pks[0] = stats[...].T[0:8]
    for n, vector in enumerate((gain_1, bias_1, gain_2, bias_2)):
        pks[0, 2 + n : 3 + n, :] = vector[...].reshape(1, 512)
    packed = [net.remote(pks.at[0], pks.at[j], net.z[j]) for j in (1, 2, 3)]
    for weight in (qkv, dense, fc):
        weight.place_own()
    bias[...] = jnp.zeros_like(bias)
    bias[3:4, 0 : b_qkv.shape[0]] = b_qkv[...].reshape(1, b_qkv.shape[0])
    bias[4:5, :] = b_fc[...].reshape(1, width)
    rows[...] = jnp.zeros_like(rows)
    load_og.wait()

    def local_grad(n, _):
        at = span(n * step, step)
        block = probs[1, at, :]
        ys[0, at, :] = block.astype(bf16)
        bias[1:2, 0:512] += jnp.sum(block, axis=0, keepdims=True)
        return 0

    lax.fori_loop(0, tok // step, local_grad, 0)
    for pack in packed:
        pack.wait_recv()
    means = [pks[j, 0:1, :] for j in range(4)]
    mu = (means[0] + means[1] + means[2] + means[3]) * 0.25
    spread = [pks[j, 1:2, :] + (means[j] - mu) * (means[j] - mu) for j in range(4)]
    rows[0:1, :] = mu
    rows[1:2, :] = lax.rsqrt((spread[0] + spread[1] + spread[2] + spread[3]) * 0.25 + epsilon)
    stats[...] = rows[...].T

    def own_norm(n, _):
        at = span(n * step, step)
        hats = (probs[0, at, :] - stats[at, 0:1]) * stats[at, 1:2]
        xs[0, at, :] = (hats * pks[0, 2:3, :] + pks[0, 3:4, :]).astype(bf16)
        return 0

    lax.fori_loop(0, tok // step, own_norm, 0)
    x_line = Line(net, xs)
    y_line = Line(net, ys)
    x_line.start()
    qkv.forward()
    x_line.step(0)
    x_line.step(1)
    fc.send_own()
    dense.forward()
    qkv.swap_near()
    x_line.step(2)
    y_line.start()
    dense.swap_near()
    qkv.swap_far()
    dense.swap_far()
    x_line.ready()

    for s in range(2):
        for j in range(4):
            lanes = span(flip(s, net.k) * Q, Q)
            dest = span(net.mix(j) * Q, Q)
            wide = span(s * HALF + net.mix(j) * Q, Q)
            vecs[0:4, wide] = pks[j, 2:6, lanes]

            def norm(n, _, s=s, j=j, lanes=lanes, dest=dest, wide=wide):
                at = span(n * step, step)
                one = xs[j, at, lanes]
                hats = (one.astype(f32) - pks[j, 3:4, lanes]) * (1.0 / pks[j, 2:3, lanes])
                xh[at, wide] = hats.astype(bf16)
                (h1s if s else h1c)[at, dest] = one
                two = hats * pks[j, 4:5, lanes] + pks[j, 5:6, lanes]
                (h2s if s else h2c)[at, dest] = two.astype(bf16)
                return 0

            lax.fori_loop(0, tok // step, norm, 0)
    swap_h1 = net.remote(h1s, h1c.at[theirs, :], net.core)
    swap_h2 = net.remote(h2s, h2c.at[theirs, :], net.core)
    fc.forward()
    proj.send_own()
    y_line.step(0)
    qkv.ready()

    def project(n, _):
        cols = span(n * 3 * HD, 3 * HD)
        acc = mm(h1c[mine, :], g_qkv[0:HALF, cols]) + mm(h1s[...], g_qkv[HALF:, cols])
        acc = acc + bias[3:4, cols]
        qb[n, :, 0:128] = turn(acc[:, 0:128], tables, 1.0).astype(bf16)
        qb[n, :, 128:HD] = acc[:, 128:HD].astype(bf16)
        kb[n, :, 0:128] = turn(acc[:, HD : HD + 128], tables, 1.0).astype(bf16)
        kb[n, :, 128:HD] = acc[:, HD + 128 : 2 * HD].astype(bf16)
        vb[n] = acc[:, 2 * HD :].astype(bf16)
        return 0

    lax.fori_loop(0, heads, project, 0)
    y_line.step(1)
    chunks = tok // step

    def attend(n, _):
        head, chunk = n // chunks, n % chunks
        at = span(chunk * step, step)
        scores = mm_nt(qb[head, at, :], kb[head]) * scale
        token = lax.broadcasted_iota(jnp.int32, (step, tok), 0) + chunk * step
        allowed = token >= lax.broadcasted_iota(jnp.int32, (step, tok), 1)
        scores = jnp.where(allowed, scores, -1e30)
        top = jnp.max(scores, axis=1, keepdims=True)
        raised = jnp.where(allowed, jnp.exp(scores - top), 0.0)
        weight = raised / jnp.sum(raised, axis=1, keepdims=True)
        probs[head, at, :] = weight
        low = weight.astype(bf16)
        probs_low[head, at, :] = low
        oc[at, span(head * HD, HD)] = mm(low, vb[head]).astype(bf16)
        return 0

    lax.fori_loop(0, heads * chunks, attend, 0)
    swap_o = net.remote(oc.at[mine, :], oc.at[theirs, :], net.core)
    fc.swap_near()
    y_line.step(2)
    fc.swap_far()
    fc.ready()

    def expand(n, _):
        cols = span(n * 512, 512)
        a = mm(h2c[mine, :], g_fc[0:HALF, cols]) + mm(h2s[...], g_fc[HALF:, cols])
        a = a + bias[4:5, cols]
        rise = 0.5 * (1.0 + lax.erf(a * 0.7071067811865476))
        gc[mine, cols] = (a * rise).astype(bf16)
        slope[:, cols] = (rise + a * 0.3989422804014327 * jnp.exp(-0.5 * a * a)).astype(bf16)
        return 0

    lax.fori_loop(0, width // 512, expand, 0)
    swap_g = net.remote(gc.at[mine, :], gc.at[theirs, :], net.core)
    proj.forward()
    y_line.ready()
    for s in range(2):
        for j in range(4):
            lanes = span(flip(s, net.k) * Q, Q)
            dest = span(net.mix(j) * Q, Q)
            (dys if s else dyc)[mine, dest] = ys[j, :, lanes]
    swap_dy = net.remote(dys, dyc.at[theirs, :], net.core)
    dense.ready()
    dob[...] = (
        mm_nt(dyc[mine, :], g_dense[:, 0:HALF]) + mm_nt(dys[...], g_dense[:, HALF:])
    ).astype(bf16)

    red_proj = Reduce(net, r_proj, j_proj, n_proj, f_proj, False)
    red_qkv = Reduce(net, r_qkv, j_qkv, n_qkv, f_qkv, True)
    red_fc = Reduce(net, r_fc, j_fc, n_fc, f_fc, True)
    red_dense = Reduce(net, r_dense, j_dense, n_dense, f_dense, False)
    swap_g.wait_recv()
    swap_dy.wait_recv()
    tall = width // 2
    tiles.write(
        4,
        lambda n: mm_tn(gc[:, span(n // 2 * tall, tall)], dyc[:, span(n % 2 * 512, 512)]),
        lambda n: r_proj.at[span(n // 2 * tall, tall), span(n % 2 * 512, 512)],
        tall,
    )
    proj.swap_near()
    red_proj.start()

    def keep(head, part, at, value, rotated):
        base = head * 3 * HD + part * HD
        if rotated:
            low = turn(value[:, 0:128], [tables[t, at, :] for t in range(3)], -1.0)
            dqc[at, pl.ds(pl.multiple_of(base, 128), 128)] = low.astype(bf16)
            bias[0:1, pl.ds(pl.multiple_of(base, 128), 128)] += jnp.sum(low, axis=0, keepdims=True)
            value, base, size = value[:, 128:], base + 128, 128
        else:
            size = HD
        cols = pl.ds(pl.multiple_of(base, 128), size)
        dqc[at, cols] = value.astype(bf16)
        bias[0:1, cols] += jnp.sum(value, axis=0, keepdims=True)

    def attend_back(head, _):
        cols = span(head * HD, HD)

        def chunk_back(n, _):
            at = span(n * step, step)
            grad = dob[at, cols]
            delta = jnp.sum(grad.astype(f32) * oc[at, cols].astype(f32), axis=1, keepdims=True)
            spread = mm_nt(grad, vb[head]) - delta
            low = (probs[head, at, :] * spread * scale).astype(bf16)
            score_low[at, :] = low
            keep(head, 0, at, mm(low, kb[head]), True)
            return 0

        lax.fori_loop(0, chunks, chunk_back, 0)
        keep(head, 1, mine, mm_tn(score_low[...], qb[head]), True)
        keep(head, 2, mine, mm_tn(probs_low[head], dob[:, cols]), False)
        return 0

    lax.fori_loop(0, heads, attend_back, 0)
    swap_dq = net.remote(dqc.at[mine, :], dqc.at[theirs, :], net.core)
    swap_o.wait_recv()
    attn = oc.shape[1]
    tiles.write(
        2,
        lambda n: mm_tn(oc[...], dyc[:, span(n * 512, 512)]),
        lambda n: r_dense.at[:, span(n * 512, 512)],
        attn,
    )
    swap_h1.wait_recv()
    swap_dq.wait_recv()
    tiles.write(
        dqc.shape[1] // 512,
        lambda n: mm_tn(h1c[...], dqc[:, span(n * 512, 512)]),
        lambda n: r_qkv.at[:, span(n * 512, 512)],
        HALF,
    )
    red_qkv.start()
    proj.swap_far()

    net.sent(swap_h1)
    net.sent(swap_h2)
    for s in range(2):

        def back_first(n, _, s=s):
            wide = span(s * HALF + n * 512, 512)
            grad = mm_nt(dqc[mine, :], g_qkv[wide, :])
            (h2s if s else h1s)[:, span(n * 512, 512)] = (grad * vecs[0:1, wide]).astype(bf16)
            vecs[4:5, wide] = jnp.sum(grad * xh[:, wide].astype(f32), axis=0, keepdims=True)
            vecs[5:6, wide] = jnp.sum(grad, axis=0, keepdims=True)
            return 0

        lax.fori_loop(0, HALF // 512, back_first, 0)

    proj.ready()
    qkv.release()
    loads = [
        net.local(w_proj.at[:, span(net.k * Q, Q)], g_qkv.at[:, pl.ds(0, Q)]),
        net.local(w_proj.at[:, span((1 - net.k) * Q, Q)], g_qkv.at[:, pl.ds(HALF, Q)]),
        net.local(all_proj.at[:, pl.ds(Q, 3 * Q)], g_qkv.at[:, pl.ds(Q, 3 * Q)]),
        net.local(all_proj.at[:, pl.ds(5 * Q, Q)], g_qkv.at[:, pl.ds(5 * Q, Q)]),
        net.local(all_proj.at[:, pl.ds(6 * Q, 2 * Q)], g_tail),
    ]
    for copy in loads:
        copy.wait()
    x_line.drain()
    y_line.drain()

    def put_out(p, product):
        s, i = p // 4, p % 4
        out = product + mm(oc[mine, :], g_dense[:, span(p * Q, Q)])
        xs[net.mix(i), :, span(flip(s, net.k) * Q, Q)] = out.astype(bf16)

    def project_head(p, _):
        put_out(p, mm(gc[mine, :], g_qkv[:, span(p * Q, Q)]))
        return 0

    def project_tail(p, _):
        put_out(6 + p, mm(gc[mine, :], g_tail[:, span(p * Q, Q)]))
        return 0

    lax.fori_loop(0, 6, project_head, 0)
    lax.fori_loop(0, 2, project_tail, 0)
    out_copies = [net.remote(xs.at[j], out_recv.at[j - 1], net.z[j]) for j in (1, 2, 3)]

    def back_fc(n, _):
        cols = span(n * 512, 512)
        grad = mm_nt(dyc[mine, :], g_qkv[cols, 0:HALF])
        grad = grad + mm_nt(dys[:, 0:512], g_qkv[cols, HALF : 6 * Q])
        grad = grad + mm_nt(dys[:, 512:], g_tail[cols, :])
        grad = grad * slope[:, cols].astype(f32)
        bias[2:3, cols] = jnp.sum(grad, axis=0, keepdims=True)
        slope[:, cols] = grad.astype(bf16)
        return 0

    lax.fori_loop(0, width // 512, back_fc, 0)
    dab = slope
    swap_da = net.remote(dab, dabt, net.core)
    red_proj.join([g_tail.at[pl.ds(0, tall), pl.ds(0, Q)], g_tail.at[pl.ds(tall, tall), pl.ds(0, Q)]])
    stats[...] = jnp.zeros_like(stats)
    lane = lax.broadcasted_iota(jnp.int32, (tok, 128), 1)

    def back_norm(j, _):
        for s in range(2):
            lanes = span(flip(s, net.k) * Q, Q)
            dest = span(net.mix(j) * Q, Q)
            wide = span(s * HALF + net.mix(j) * Q, Q)
            grad = mm_nt(dab[...], g_fc[wide, :])
            hats = xh[:, wide].astype(f32)
            packs[j, 2:4, lanes] = vecs[4:6, wide]
            packs[j, 4:5, lanes] = jnp.sum(grad * hats, axis=0, keepdims=True)
            packs[j, 5:6, lanes] = jnp.sum(grad, axis=0, keepdims=True)
            joint = (h2s if s else h1s)[:, dest].astype(f32) + grad * vecs[2:3, wide]
            ys[j, :, lanes] = joint.astype(bf16)
            one = jnp.sum(joint, axis=1, keepdims=True)
            two = jnp.sum(joint * hats, axis=1, keepdims=True)
            stats[...] += jnp.where(lane == 0, one, jnp.where(lane == 1, two, 0.0))
        return 0

    lax.fori_loop(0, 4, back_norm, 0)
    turned = stats[...].T
    for j in range(4):
        packs[j, 0:2, :] = turned[0:2]
        packs[j, 6:8, :] = jnp.zeros((2, tok), f32)
    pack_copies = [net.remote(packs.at[j], packs.at[3 + j], net.z[j]) for j in (1, 2, 3)]
    hat_copies = [net.remote(ys.at[j], hat_recv.at[j - 1], net.z[j]) for j in (1, 2, 3)]
    swap_h2.wait_recv()
    swap_da.wait_recv()

    def grad_fc(n):
        cols = span(n * 512, 512)
        return mm_tn(h2c[mine, :], dab[:, cols]) + mm_tn(h2c[theirs, :], dabt[:, cols])

    tiles.write(width // 512, grad_fc, lambda n: r_fc.at[:, span(n * 512, 512)], HALF)
    red_fc.start()

    fc.release()

    def strips(base, n, columns):
        return g_fc.at[pl.ds(base + n * Q, Q), pl.ds(0, columns)]

    halves = [g_fc.at[pl.ds(7 * Q + n * (Q // 2), Q // 2), pl.ds(0, 6 * Q)] for n in range(2)]
    red_qkv.join(halves)
    red_dense.start()
    red_proj.finish([g_qkv.at[:, pl.ds(n * Q, Q)] for n in range(4)], o_proj)
    for copy in pack_copies:
        copy.wait_recv()
    total = packs[0] + packs[4] + packs[5] + packs[6]
    rows[2:4, :] = total[0:2, :]
    o_stats[...] = rows[...].T
    small[0, 0:4, :] = total[2:6, :]
    for n in range(3):
        small[0, 4 + n : 5 + n, :] = bias[0:1, n * 512 : n * 512 + 512]
    for n in range(4):
        small[0, 7 + n : 8 + n, :] = bias[2:3, n * 512 : n * 512 + 512]
    small[0, 11:12, :] = bias[1:2, 0:512]
    small[0, 12:16, :] = jnp.zeros((4, 512), f32)
    for hop, peer in enumerate((net.core, net.x, net.y)):
        net.remote(small.at[hop], small.at[4 + hop], peer).wait_recv()
        small[hop + 1] = small[hop] + small[4 + hop]
    o_small[...] = small[3]

    def sum_blocks(sent, received, total):
        def body(n, _):
            at = span(n * 64, 64)
            value = sent[0, at, :].astype(f32)
            for j in range(3):
                value = value + received[j, at, :].astype(f32)
            total[at, :] = value
            return 0

        lax.fori_loop(0, tok // 64, body, 0)

    for copy in out_copies:
        copy.wait_recv()
    sum_blocks(xs, out_recv, probs.at[0])
    keep_branch = net.local(probs.at[0], o_branch)
    red_fc.join([g_fc.at[pl.ds(6 * Q + n * (Q // 2), Q // 2), :] for n in range(2)])
    red_qkv.finish([strips(0, n, 6 * Q) for n in range(4)], o_qkv)
    dense_parts = [g_tail.at[pl.ds(n * attn, attn), pl.ds(Q, Q)] for n in range(4)]
    red_dense.join([g_tail.at[pl.ds(n * attn // 2, attn // 2), pl.ds(0, Q)] for n in range(2)])
    red_fc.finish([strips(4 * Q, n, 8 * Q) for n in range(4)], o_fc)
    red_dense.finish(dense_parts, o_dense)
    for copy in hat_copies:
        copy.wait_recv()
    sum_blocks(ys, hat_recv, probs.at[1])
    keep_hat = net.local(probs.at[1], o_hat)
    for weight in (red_proj, red_qkv, red_fc, red_dense):
        weight.done()
    keep_branch.wait()
    keep_hat.wait()
    net.drain()


def call_block(*args):
    x, w_qkv, w_dense = args[0], args[6], args[7]
    tok = x.shape[0]
    n_qkv, n_attn, n_fc = w_qkv.shape[1], w_dense.shape[0], args[8].shape[1]
    heads = n_attn // HD
    wide = 2 * HALF
    any_spec = pl.BlockSpec(memory_space=pl.ANY)
    vmem = pl.BlockSpec(memory_space=VMEM)
    shape = jax.ShapeDtypeStruct
    pieces = ((n_fc, Q), (Q, n_qkv), (Q, n_fc), (n_attn, Q))
    outs = [
        shape((n_fc, 2 * Q), bf16), shape((2 * Q, n_qkv), bf16),
        shape((2 * Q, n_fc), bf16), shape((n_attn, 2 * Q), bf16),
        shape((tok, 512), f32), shape((tok, 512), f32),
        shape((n_fc, wide), bf16), shape((n_fc, HALF), bf16), shape((HALF, n_qkv), bf16),
        shape((HALF, n_fc), bf16), shape((n_attn, HALF), bf16),
    ]
    outs += [shape(piece, bf16) for piece in pieces for _ in range(2)]
    outs += [shape((tok, 128), f32), shape((16, 512), f32)]
    scratch = [
        VMEM((wide, n_qkv), bf16), VMEM((n_attn, wide), bf16), VMEM((wide, n_fc), bf16),
        VMEM((n_fc, 2 * Q), bf16),
        VMEM((4, tok, 512), bf16), VMEM((4, tok, 512), bf16), VMEM((4, 8, tok), f32),
        VMEM((tok, 128), f32), VMEM((128, tok), f32),
        VMEM((2 * tok, HALF), bf16), VMEM((tok, HALF), bf16),
        VMEM((2 * tok, HALF), bf16), VMEM((tok, HALF), bf16),
        VMEM((2 * tok, HALF), bf16), VMEM((tok, HALF), bf16), VMEM((tok, wide), bf16),
        VMEM((heads, tok, HD), bf16), VMEM((heads, tok, HD), bf16), VMEM((heads, tok, HD), bf16),
        VMEM((heads, tok, tok), f32), VMEM((heads, tok, tok), bf16), VMEM((tok, tok), bf16),
        VMEM((2 * tok, n_attn), bf16), VMEM((tok, n_attn), bf16), VMEM((2 * tok, n_qkv), bf16),
        VMEM((2 * tok, n_fc), bf16), VMEM((tok, n_fc), bf16), VMEM((tok, n_fc), bf16),
        VMEM((2, HALF, 512), bf16),
        VMEM((3, tok, 512), bf16), VMEM((3, tok, 512), bf16),
    ]
    scratch += [VMEM((2,) + ((r // 2, c)), bf16) for r, c in pieces]
    scratch += [
        VMEM((8, wide), f32), VMEM((8, n_fc), f32), VMEM((7, 8, tok), f32), VMEM((7, 16, 512), f32),
        pltpu.SemaphoreType.DMA((96,)), pltpu.SemaphoreType.DMA((96,)),
        pltpu.SemaphoreType.DMA((64,)), pltpu.SemaphoreType.DMA((2,)),
    ]
    return pl.pallas_call(
        block_kernel,
        name="block",
        out_shape=outs,
        in_specs=[any_spec] * 2 + [vmem] * 4 + [any_spec] * 4 + [vmem] * 3,
        out_specs=[any_spec] * 19 + [vmem] * 2,
        scratch_shapes=scratch,
        compiler_params=pltpu.CompilerParams(
            collective_id=1, has_side_effects=True, vmem_limit_bytes=67043328
        ),
    )(*args)


def turn_tables(length):
    half_rot = ROT // 2
    frequency = (10000.0 ** (-np.arange(half_rot, dtype=np.float32) * (2.0 / ROT))).astype(np.float32)
    angles = np.arange(length, dtype=np.float32)[:, None] * frequency[None, :]
    tables = np.zeros((3, length, 128), np.float32)
    tables[0] = 1.0
    tables[0, :, :half_rot] = tables[0, :, half_rot:ROT] = np.cos(angles)
    tables[1, :, :half_rot] = -np.sin(angles)
    tables[2, :, half_rot:ROT] = np.sin(angles)
    return tables


def fused_shards(
    block_input, out_grad, ln1_gain, ln1_bias, ln2_gain, ln2_bias,
    w_qkv, b_qkv, w_dense, b_dense, w_fc, b_fc, w_proj, b_proj,
):
    results = call_block(
        block_input, out_grad, ln1_gain, ln1_bias, ln2_gain, ln2_bias,
        w_qkv, w_dense, w_fc, w_proj, b_qkv, b_fc, turn_tables(SEQ),
    )
    proj_total, qkv_total, fc_total, dense_total = (part.astype(f32) for part in results[:4])
    branch, hat_grad = results[4:6]
    stats, small = results[19:]
    mu, rstd, total, cross = (stats[:, n : n + 1] for n in range(4))
    block_output = block_input + branch + (b_dense + b_proj)
    x_hat = (block_input - mu) * rstd
    input_grad = out_grad + rstd * (hat_grad - total * (1.0 / D) - x_hat * (cross * (1.0 / D)))
    return (
        block_output, input_grad, small[0], small[1], small[2], small[3],
        qkv_total, small[4:7].reshape(-1), dense_total, small[11],
        fc_total, small[7:11].reshape(-1), proj_total, small[11],
    )


def solution(mesh):
    sizes = tuple(mesh.shape[name] for name in ("dp", "row", "col"))
    body = fused_shards if sizes == (2, 4, 4) else shards
    return jax.shard_map(
        body,
        mesh=mesh,
        in_specs=(
            P(("dp", "row"), "col"),
            P(("dp", "row"), "col"),
            P("col"),
            P("col"),
            P("col"),
            P("col"),
            P("row", "col"),
            P("col"),
            P("col", "row"),
            P("col"),
            P("row", "col"),
            P("col"),
            P("col", "row"),
            P("col"),
        ),
        out_specs=(
            P(("dp", "row"), "col"),
            P(("dp", "row"), "col"),
            P("col"),
            P("col"),
            P("col"),
            P("col"),
            P("row", "col"),
            P("col"),
            P("col", "row"),
            P("col"),
            P("row", "col"),
            P("col"),
            P("col", "row"),
            P("col"),
        ),
        check_vma=False,
    )
```

time: 268 us -> 245 us (0.914)
  Pallas kernels: 246 us -> 225 us
  local copies, waits for them, and re-layouts: 13.4 us -> 2.42 us
  other arithmetic: 7.8 us -> 15 us
    pallas_call x2 -> x1, Pallas kernels: 246 us -> 225 us  [call_block(): pl.pallas_call(block_kernel, name='block', out_shape=outs, in_specs=[any_...]
    unnamed x19 -> x15, local copies, waits for them, and re-layouts: 10.9 us -> 1.21 us
    convert_element_type x0 -> x4, other arithmetic: none -> 8.32 us  [fused_shards(): part.astype(f32)]
where the time goes in v2:
time: 245 us; the launch traced here: 243 us
  Pallas kernels  225 us (92%)
  other arithmetic  15 us (6%)
    pallas_call x1, Pallas kernels, call_block(): pl.pallas_call(block_kernel, name='block', out_shape=outs, in_specs=[any_...  225 us
    convert_element_type x4, other arithmetic, fused_shards(): part.astype(f32)  8.32 us

profile of v2, /device:TPU:1, one launch (start us, length us, event | category | flops | bytes accessed | tf_op | source)
XLA Modules:
  0.0 242.9 jit_solution(17546153119808976025)
XLA Ops:
  0.6 224.9 %block.1 = (bf16[2048,512]{1,0:T(8,128)(2,1)}, bf16[512,1536]{1,0:T(8,128)(2,1)}, bf16[512,2048]{1,0:T(8,128)(2,1)}, bf16[512,512]{1,0:T(8,128)(2,1)}, f32[512,5...) custom-call(f32[512,512]{1,0:T(8,128)} %x.1, ...), custom_call_target="tpu_custom_call" | custom-call | tf_op jit(solution)/shard_map/block/pallas_call | solution.py:1066
  225.5 2.0 slice_reduce_fusion.1
  227.5 0.7 add.18
  228.2 0.0 copy-start.4
  228.2 0.0 copy-start.1
  228.2 4.0 %multiply_add_fusion = (f32[512,512]{1,0:T(8,128)}, f32[512,512]{1,0:T(8,128)}) fusion(f32[512,512]{1,0:T(8,128)} %og.1, f32[512,512]{1,0:T(8,128)} %x.1, f32[512,512]{1,0:T(8,128)} %get-tuple-element.24, f32[512]{0:T(512)S(1)} %get-tuple-element.31, f32[512]{0:T(512)S(1)} %get-tuple-element.32, f32[512]{0:T(512)S(1)} %get-tuple-element.33, ...), kind=kLoop, calls=%fused_computation | loop fusion | flops 2359296 | bytes 6301696 | tf_op jit(solution)/shard_map/add | solution.py:1105
  232.2 0.0 copy-done.4
  232.2 0.6 fusion
  232.8 0.0 copy-start.5
  232.8 0.6 copy.29
  233.4 0.6 reshape.35
  234.0 0.0 copy-done.1
  234.0 0.0 copy-start
  234.0 2.5 %convert_element_type.14 = f32[512,2048]{1,0:T(8,128)} convert(bf16[512,2048]{1,0:T(8,128)(2,1)S(1)} %copy-done.1) | non-fusion elementwise | flops 1048576 | bytes 6291456 | tf_op jit(solution)/shard_map/convert_element_type | solution.py:1099
  236.5 0.0 copy-done
  236.6 0.0 copy-start.2
  236.6 2.6 %convert_element_type.15 = f32[2048,512]{1,0:T(8,128)} convert(bf16[2048,512]{1,0:T(8,128)(2,1)S(1)} %copy-done) | non-fusion elementwise | flops 1048576 | bytes 6291456 | tf_op jit(solution)/shard_map/convert_element_type | solution.py:1099
  239.2 0.0 copy-start.3
  239.2 0.0 copy-done.2
  239.2 2.1 convert_element_type.12
  241.2 0.0 copy-done.3
  241.2 1.1 convert_element_type.13
  242.3 0.0 copy-done.5
  242.3 0.6 copy.31
  (2 shorter events, 0.0 us)
Async XLA Ops:
  228.2 4.0 %copy-start.4 = (f32[16,512]{1,0:T(8,128)S(1)}, f32[16,512]{1,0:T(8,128)}, u32[]{:S(2)}) copy-start(f32[16,512]{1,0:T(8,128)} %get-tuple-element.25) | copy-start | bytes 98308
  228.2 5.8 %copy-start.1 = (bf16[512,2048]{1,0:T(8,128)(2,1)S(1)}, bf16[512,2048]{1,0:T(8,128)(2,1)}, u32[]{:S(2)}) copy-start(bf16[512,2048]{1,0:T(8,128)(2,1)} %get-tuple-element.28) | copy-start | bytes 6291460
  232.8 9.6 %copy-start.5 = (f32[1,512]{1,0:T(1,128)}, f32[1,512]{1,0:T(1,128)S(1)}, u32[]{:S(2)}) copy-start(f32[1,512]{1,0:T(1,128)S(1)} %get-tuple-element.36) | copy-start | bytes 6148
  234.0 2.5 %copy-start = (bf16[2048,512]{1,0:T(8,128)(2,1)S(1)}, bf16[2048,512]{1,0:T(8,128)(2,1)}, u32[]{:S(2)}) copy-start(bf16[2048,512]{1,0:T(8,128)(2,1)} %get-tuple-element.29) | copy-start | bytes 6291460
  236.6 2.6 %copy-start.2 = (bf16[512,1536]{1,0:T(8,128)(2,1)S(1)}, bf16[512,1536]{1,0:T(8,128)(2,1)}, u32[]{:S(2)}) copy-start(bf16[512,1536]{1,0:T(8,128)(2,1)} %get-tuple-element.26) | copy-start | bytes 4718596
  239.2 2.1 copy-start.3

commit v3 on v2

--- a/solution.py
+++ b/solution.py
@@ -513,9 +513,86 @@
                 hop.wait_send()
 
 
+class Fold:
+    def __init__(self, net, blocks, inbox):
+        self.net, self.blocks, self.inbox = net, blocks, inbox
+        hops = ((3, None, 0), (2, None, 1), (1, None, 2), (None, 0, 3), (None, 1, 4), (None, 3, 0))
+        self.copies = []
+        for n, (block, slot, dest) in enumerate(hops):
+            number = net.slot()
+            self.copies.append(
+                pltpu.make_async_remote_copy(
+                    src_ref=blocks.at[block] if slot is None else inbox.at[slot],
+                    dst_ref=inbox.at[dest],
+                    send_sem=net.send_sems.at[number],
+                    recv_sem=net.recv_sems.at[number],
+                    device_id=net.z[3] if n in (3, 4) else net.z[1],
+                    device_id_type=MESH,
+                )
+            )
+
+    def start(self):
+        @pl.when(jnp.logical_not(self.net.middle))
+        def _():
+            for copy in self.copies[:3]:
+                copy.start()
+
+    def step(self, number):
+        slot, block = ((0, 2), (1, 3), (3, 1))[number]
+        inbox, blocks = self.inbox, self.blocks
+
+        @pl.when(self.net.middle)
+        def _():
+            self.copies[(0, 1, 3)[number]].wait_recv()
+
+            def add(n, _):
+                at = span(n * 64, 64)
+                total = inbox[slot, at, :].astype(f32) + blocks[block, at, :].astype(f32)
+                inbox[slot, at, :] = total.astype(bf16)
+                return 0
+
+            lax.fori_loop(0, inbox.shape[1] // 64, add, 0)
+            self.copies[3 + number].start()
+
+    def total(self, use):
+        def gather(*slots):
+            def add(n, _):
+                at = span(n * 64, 64)
+                value = self.blocks[0, at, :].astype(f32)
+                for slot in slots:
+                    value = value + self.inbox[slot, at, :].astype(f32)
+                use(at, value)
+                return 0
+
+            lax.fori_loop(0, self.inbox.shape[1] // 64, add, 0)
+
+        @pl.when(self.net.middle)
+        def _():
+            self.copies[2].wait_recv()
+            self.copies[4].wait_recv()
+            gather(2, 4)
+
+        @pl.when(jnp.logical_not(self.net.middle))
+        def _():
+            self.copies[5].wait_recv()
+            gather(0)
+
+    def drain(self):
+        @pl.when(self.net.middle)
+        def _():
+            for copy in self.copies[3:]:
+                copy.wait_send()
+
+        @pl.when(jnp.logical_not(self.net.middle))
+        def _():
+            for copy in self.copies[:3]:
+                copy.wait_send()
+
+
 def turn(low, tables, sign):
-    swing = tables[1] * pltpu.roll(low, 96, 1) + tables[2] * pltpu.roll(low, 32, 1)
-    return low * tables[0] + sign * swing
+    lane = lax.broadcasted_iota(jnp.int32, low.shape, 1)
+    swung = jnp.where(lane < ROT // 2, pltpu.roll(low, 96, 1), pltpu.roll(low, 32, 1))
+    return low * tables[0] + sign * (tables[1] * swung)
 
 
 class Tiles:
@@ -543,7 +620,8 @@
 
 
 class Reduce:
-    def __init__(self, net, partial, joined, near, far, by_rows):
+    def __init__(self, net, partial, joined, near, far, by_rows, in_vmem=False):
+        self.in_vmem = in_vmem
         self.net, self.partial, self.by_rows = net, partial, by_rows
         self.joined, self.near, self.far = joined, near, far
         self.depth = Q // 2 if by_rows else partial.shape[0] // 2
@@ -587,16 +665,24 @@
             hops.append(net.remote(self.joined.at[half], self.far.at[self.rows(half), :], peer))
         self.far_a, self.far_b = hops
 
-    def finish(self, buffers, out):
+    def prepare(self, buffers):
         net = self.net
-        loads = [net.local(self.whole(), buffers[0])]
+        self.buffers = list(buffers)
+        self.loads = [net.local(self.whole(), buffers[0])]
         for copy in (self.near_a, self.near_b):
             copy.wait_recv()
-        loads.append(net.local(self.near, buffers[1]))
+        if self.in_vmem:
+            self.buffers[1:3] = [self.near, self.far]
+        else:
+            self.loads.append(net.local(self.near, buffers[1]))
+
+    def finish(self, out):
+        net, buffers = self.net, self.buffers
         for copy in (self.far_a, self.far_b):
             copy.wait_recv()
-        loads.append(net.local(self.far, buffers[2]))
-        for copy in loads:
+        if not self.in_vmem:
+            self.loads.append(net.local(self.far, buffers[2]))
+        for copy in self.loads:
             copy.wait()
         tile = 64
 
@@ -620,14 +706,13 @@
 
 
 def block_kernel(
-    x, og, gain_1, bias_1, gain_2, bias_2, w_qkv, w_dense, w_fc, w_proj, b_qkv, b_fc, tables,
-    o_proj, o_qkv, o_fc, o_dense, o_branch, o_hat,
-    all_proj, r_proj, r_qkv, r_fc, r_dense,
-    n_proj, f_proj, n_qkv, f_qkv, n_fc, f_fc, n_dense, f_dense,
-    o_stats, o_small,
+    x, og, w_qkv, w_dense, w_fc, w_proj, t_turn,
+    gain_1, bias_1, gain_2, bias_2, b_qkv, b_fc, b_dense, b_proj,
+    o_proj, o_qkv, o_fc, o_dense, o_block, o_input, o_small,
+    all_proj, r_proj, r_qkv, r_fc, r_dense, n_proj, f_proj, n_qkv, f_qkv, n_fc, f_fc,
     g_qkv, g_dense, g_fc, g_tail, xs, ys, pks, stats, rows, h1c, h1s, h2c, h2s, dyc, dys, xh,
-    qb, kb, vb, probs, probs_low, score_low, oc, dob, dqc, gc, slope, dabt, stage,
-    out_recv, hat_recv, j_proj, j_qkv, j_fc, j_dense, vecs, bias, packs, small,
+    qb, kb, vb, probs, probs_low, oc, dob, dqc, gc, slope, dabt, stage,
+    out_recv, hat_recv, j_proj, j_qkv, j_fc, j_dense, n_dense, f_dense, tables, vecs, bias, packs, small,
     send_sems, recv_sems, local_sems, stage_sems,
 ):
     tok = x.shape[0]
@@ -644,6 +729,7 @@
     dense.send_own()
     load_x = net.local(x, probs.at[0])
     load_og = net.local(og, probs.at[1])
+    load_turn = net.local(t_turn, tables)
     tiles = Tiles(stage, stage_sems)
     mine = pl.ds(0, tok)
     theirs = pl.ds(tok, tok)
@@ -671,6 +757,7 @@
     bias[...] = jnp.zeros_like(bias)
     bias[3:4, 0 : b_qkv.shape[0]] = b_qkv[...].reshape(1, b_qkv.shape[0])
     bias[4:5, :] = b_fc[...].reshape(1, width)
+    bias[5:6, 0:512] = (b_dense[...] + b_proj[...]).reshape(1, 512)
     rows[...] = jnp.zeros_like(rows)
     load_og.wait()
 
@@ -737,6 +824,7 @@
     fc.forward()
     proj.send_own()
     y_line.step(0)
+    load_turn.wait()
     qkv.ready()
 
     def project(n, _):
@@ -804,7 +892,7 @@
     red_proj = Reduce(net, r_proj, j_proj, n_proj, f_proj, False)
     red_qkv = Reduce(net, r_qkv, j_qkv, n_qkv, f_qkv, True)
     red_fc = Reduce(net, r_fc, j_fc, n_fc, f_fc, True)
-    red_dense = Reduce(net, r_dense, j_dense, n_dense, f_dense, False)
+    red_dense = Reduce(net, r_dense, j_dense, n_dense, f_dense, False, True)
     swap_g.wait_recv()
     swap_dy.wait_recv()
     tall = width // 2
@@ -820,7 +908,7 @@
     def keep(head, part, at, value, rotated):
         base = head * 3 * HD + part * HD
         if rotated:
-            low = turn(value[:, 0:128], [tables[t, at, :] for t in range(3)], -1.0)
+            low = turn(value[:, 0:128], [tables[t, at, :] for t in range(2)], -1.0)
             dqc[at, pl.ds(pl.multiple_of(base, 128), 128)] = low.astype(bf16)
             bias[0:1, pl.ds(pl.multiple_of(base, 128), 128)] += jnp.sum(low, axis=0, keepdims=True)
             value, base, size = value[:, 128:], base + 128, 128
@@ -839,36 +927,17 @@
             delta = jnp.sum(grad.astype(f32) * oc[at, cols].astype(f32), axis=1, keepdims=True)
             spread = mm_nt(grad, vb[head]) - delta
             low = (probs[head, at, :] * spread * scale).astype(bf16)
-            score_low[at, :] = low
+            probs_low[head, at, :] = low
             keep(head, 0, at, mm(low, kb[head]), True)
             return 0
 
+        keep(head, 2, mine, mm_tn(probs_low[head], dob[:, cols]), False)
         lax.fori_loop(0, chunks, chunk_back, 0)
-        keep(head, 1, mine, mm_tn(score_low[...], qb[head]), True)
-        keep(head, 2, mine, mm_tn(probs_low[head], dob[:, cols]), False)
+        keep(head, 1, mine, mm_tn(probs_low[head], qb[head]), True)
         return 0
 
     lax.fori_loop(0, heads, attend_back, 0)
     swap_dq = net.remote(dqc.at[mine, :], dqc.at[theirs, :], net.core)
-    swap_o.wait_recv()
-    attn = oc.shape[1]
-    tiles.write(
-        2,
-        lambda n: mm_tn(oc[...], dyc[:, span(n * 512, 512)]),
-        lambda n: r_dense.at[:, span(n * 512, 512)],
-        attn,
-    )
-    swap_h1.wait_recv()
-    swap_dq.wait_recv()
-    tiles.write(
-        dqc.shape[1] // 512,
-        lambda n: mm_tn(h1c[...], dqc[:, span(n * 512, 512)]),
-        lambda n: r_qkv.at[:, span(n * 512, 512)],
-        HALF,
-    )
-    red_qkv.start()
-    proj.swap_far()
-
     net.sent(swap_h1)
     net.sent(swap_h2)
     for s in range(2):
@@ -883,6 +952,7 @@
 
         lax.fori_loop(0, HALF // 512, back_first, 0)
 
+    proj.swap_far()
     proj.ready()
     qkv.release()
     loads = [
@@ -892,6 +962,25 @@
         net.local(all_proj.at[:, pl.ds(5 * Q, Q)], g_qkv.at[:, pl.ds(5 * Q, Q)]),
         net.local(all_proj.at[:, pl.ds(6 * Q, 2 * Q)], g_tail),
     ]
+    swap_o.wait_recv()
+    attn = oc.shape[1]
+    tiles.write(
+        2,
+        lambda n: mm_tn(oc[...], dyc[:, span(n * 512, 512)]),
+        lambda n: r_dense.at[:, span(n * 512, 512)],
+        attn,
+    )
+    swap_h1.wait_recv()
+    swap_dq.wait_recv()
+    tiles.write(
+        dqc.shape[1] // 512,
+        lambda n: mm_tn(h1c[...], dqc[:, span(n * 512, 512)]),
+        lambda n: r_qkv.at[:, span(n * 512, 512)],
+        HALF,
+    )
+    red_qkv.start()
+    red_dense.start()
+
     for copy in loads:
         copy.wait()
     x_line.drain()
@@ -912,7 +1001,8 @@
 
     lax.fori_loop(0, 6, project_head, 0)
     lax.fori_loop(0, 2, project_tail, 0)
-    out_copies = [net.remote(xs.at[j], out_recv.at[j - 1], net.z[j]) for j in (1, 2, 3)]
+    out_fold = Fold(net, xs, out_recv)
+    out_fold.start()
 
     def back_fc(n, _):
         cols = span(n * 512, 512)
@@ -949,12 +1039,19 @@
         return 0
 
     lax.fori_loop(0, 4, back_norm, 0)
+
+    fc.release()
+    red_qkv.join(
+        [g_fc.at[pl.ds(7 * Q + n * (Q // 2), Q // 2), pl.ds(0, 6 * Q)] for n in range(2)]
+    )
     turned = stats[...].T
     for j in range(4):
         packs[j, 0:2, :] = turned[0:2]
         packs[j, 6:8, :] = jnp.zeros((2, tok), f32)
     pack_copies = [net.remote(packs.at[j], packs.at[3 + j], net.z[j]) for j in (1, 2, 3)]
-    hat_copies = [net.remote(ys.at[j], hat_recv.at[j - 1], net.z[j]) for j in (1, 2, 3)]
+    hat_fold = Fold(net, ys, hat_recv)
+    hat_fold.start()
+    out_fold.step(0)
     swap_h2.wait_recv()
     swap_da.wait_recv()
 
@@ -964,69 +1061,83 @@
 
     tiles.write(width // 512, grad_fc, lambda n: r_fc.at[:, span(n * 512, 512)], HALF)
     red_fc.start()
-
-    fc.release()
+    out_fold.step(1)
 
     def strips(base, n, columns):
         return g_fc.at[pl.ds(base + n * Q, Q), pl.ds(0, columns)]
 
-    halves = [g_fc.at[pl.ds(7 * Q + n * (Q // 2), Q // 2), pl.ds(0, 6 * Q)] for n in range(2)]
-    red_qkv.join(halves)
-    red_dense.start()
-    red_proj.finish([g_qkv.at[:, pl.ds(n * Q, Q)] for n in range(4)], o_proj)
+    out_fold.step(2)
     for copy in pack_copies:
         copy.wait_recv()
     total = packs[0] + packs[4] + packs[5] + packs[6]
     rows[2:4, :] = total[0:2, :]
-    o_stats[...] = rows[...].T
-    small[0, 0:4, :] = total[2:6, :]
+    stats[...] = rows[...].T
+    me = net.k * 4 + net.r
+    small[me, 0:4, :] = total[2:6, :]
     for n in range(3):
-        small[0, 4 + n : 5 + n, :] = bias[0:1, n * 512 : n * 512 + 512]
+        small[me, 4 + n : 5 + n, :] = bias[0:1, n * 512 : n * 512 + 512]
     for n in range(4):
-        small[0, 7 + n : 8 + n, :] = bias[2:3, n * 512 : n * 512 + 512]
-    small[0, 11:12, :] = bias[1:2, 0:512]
-    small[0, 12:16, :] = jnp.zeros((4, 512), f32)
-    for hop, peer in enumerate((net.core, net.x, net.y)):
-        net.remote(small.at[hop], small.at[4 + hop], peer).wait_recv()
-        small[hop + 1] = small[hop] + small[4 + hop]
-    o_small[...] = small[3]
-
-    def sum_blocks(sent, received, total):
-        def body(n, _):
-            at = span(n * 64, 64)
-            value = sent[0, at, :].astype(f32)
-            for j in range(3):
-                value = value + received[j, at, :].astype(f32)
-            total[at, :] = value
-            return 0
-
-        lax.fori_loop(0, tok // 64, body, 0)
-
-    for copy in out_copies:
+        small[me, 7 + n : 8 + n, :] = bias[2:3, n * 512 : n * 512 + 512]
+    small[me, 11:12, :] = bias[1:2, 0:512]
+    small[me, 12:16, :] = jnp.zeros((4, 512), f32)
+    small_copies = []
+    for n in range(1, 8):
+        row = flip(net.r % 2, n % 2) + 2 * flip(net.r // 2, n // 2 % 2)
+        peer = (flip(net.k, n // 4), row, net.c)
+        small_copies.append(net.remote(small.at[me], small.at[me], peer))
+    reload_x = net.local(x, probs.at[1])
+    red_proj.prepare([g_qkv.at[:, pl.ds(n * Q, Q)] for n in range(4)])
+    red_proj.finish(o_proj)
+    reload_x.wait()
+
+    def close_out(at, value):
+        probs[0, at, :] = probs[1, at, :] + value + bias[5:6, 0:512]
+
+    out_fold.total(close_out)
+    keep_block = net.local(probs.at[0], o_block)
+    hat_fold.step(0)
+    red_fc.join([g_fc.at[pl.ds(6 * Q + n * (Q // 2), Q // 2), :] for n in range(2)])
+    hat_fold.step(1)
+    hat_fold.step(2)
+    keep_block.wait()
+    reload_og = net.local(og, probs.at[0])
+    red_qkv.prepare([strips(0, n, 6 * Q) for n in range(4)])
+    red_qkv.finish(o_qkv)
+    red_dense.join([g_tail.at[pl.ds(n * attn // 2, attn // 2), pl.ds(0, Q)] for n in range(2)])
+    red_fc.prepare([strips(4 * Q, n, 8 * Q) for n in range(4)])
+    red_dense.prepare([g_tail.at[pl.ds(n * attn, attn), pl.ds(Q, Q)] for n in range(4)])
+    for copy in small_copies:
         copy.wait_recv()
-    sum_blocks(xs, out_recv, probs.at[0])
-    keep_branch = net.local(probs.at[0], o_branch)
-    red_fc.join([g_fc.at[pl.ds(6 * Q + n * (Q // 2), Q // 2), :] for n in range(2)])
-    red_qkv.finish([strips(0, n, 6 * Q) for n in range(4)], o_qkv)
-    dense_parts = [g_tail.at[pl.ds(n * attn, attn), pl.ds(Q, Q)] for n in range(4)]
-    red_dense.join([g_tail.at[pl.ds(n * attn // 2, attn // 2), pl.ds(0, Q)] for n in range(2)])
-    red_fc.finish([strips(4 * Q, n, 8 * Q) for n in range(4)], o_fc)
-    red_dense.finish(dense_parts, o_dense)
-    for copy in hat_copies:
-        copy.wait_recv()
-    sum_blocks(ys, hat_recv, probs.at[1])
-    keep_hat = net.local(probs.at[1], o_hat)
+    grand = small[0]
+    for n in range(1, 8):
+        grand = grand + small[n]
+    small[8] = grand
+    keep_small = net.local(small.at[8], o_small)
+    reload_og.wait()
+
+    def close_hat(at, value):
+        mu, rstd = stats[at, 0:1], stats[at, 1:2]
+        hats = (probs[1, at, :] - mu) * rstd
+        mean, cross = stats[at, 2:3] * (1.0 / D), stats[at, 3:4] * (1.0 / D)
+        probs[0, at, :] += rstd * (value - mean - hats * cross)
+
+    hat_fold.total(close_hat)
+    keep_input = net.local(probs.at[0], o_input)
+    red_fc.finish(o_fc)
+    red_dense.finish(o_dense)
     for weight in (red_proj, red_qkv, red_fc, red_dense):
         weight.done()
-    keep_branch.wait()
-    keep_hat.wait()
+    keep_small.wait()
+    keep_input.wait()
+    out_fold.drain()
+    hat_fold.drain()
     net.drain()
 
 
 def call_block(*args):
-    x, w_qkv, w_dense = args[0], args[6], args[7]
+    x, w_qkv, w_dense, w_fc = args[0], args[2], args[3], args[4]
     tok = x.shape[0]
-    n_qkv, n_attn, n_fc = w_qkv.shape[1], w_dense.shape[0], args[8].shape[1]
+    n_qkv, n_attn, n_fc = w_qkv.shape[1], w_dense.shape[0], w_fc.shape[1]
     heads = n_attn // HD
     wide = 2 * HALF
     any_spec = pl.BlockSpec(memory_space=pl.ANY)
@@ -1036,12 +1147,11 @@
     outs = [
         shape((n_fc, 2 * Q), bf16), shape((2 * Q, n_qkv), bf16),
         shape((2 * Q, n_fc), bf16), shape((n_attn, 2 * Q), bf16),
-        shape((tok, 512), f32), shape((tok, 512), f32),
+        shape((tok, 512), f32), shape((tok, 512), f32), shape((16, 512), f32),
         shape((n_fc, wide), bf16), shape((n_fc, HALF), bf16), shape((HALF, n_qkv), bf16),
         shape((HALF, n_fc), bf16), shape((n_attn, HALF), bf16),
     ]
-    outs += [shape(piece, bf16) for piece in pieces for _ in range(2)]
-    outs += [shape((tok, 128), f32), shape((16, 512), f32)]
+    outs += [shape(piece, bf16) for piece in pieces[:3] for _ in range(2)]
     scratch = [
         VMEM((wide, n_qkv), bf16), VMEM((n_attn, wide), bf16), VMEM((wide, n_fc), bf16),
         VMEM((n_fc, 2 * Q), bf16),
@@ -1051,24 +1161,26 @@
         VMEM((2 * tok, HALF), bf16), VMEM((tok, HALF), bf16),
         VMEM((2 * tok, HALF), bf16), VMEM((tok, HALF), bf16), VMEM((tok, wide), bf16),
         VMEM((heads, tok, HD), bf16), VMEM((heads, tok, HD), bf16), VMEM((heads, tok, HD), bf16),
-        VMEM((heads, tok, tok), f32), VMEM((heads, tok, tok), bf16), VMEM((tok, tok), bf16),
+        VMEM((heads, tok, tok), f32), VMEM((heads, tok, tok), bf16),
         VMEM((2 * tok, n_attn), bf16), VMEM((tok, n_attn), bf16), VMEM((2 * tok, n_qkv), bf16),
         VMEM((2 * tok, n_fc), bf16), VMEM((tok, n_fc), bf16), VMEM((tok, n_fc), bf16),
         VMEM((2, HALF, 512), bf16),
-        VMEM((3, tok, 512), bf16), VMEM((3, tok, 512), bf16),
+        VMEM((5, tok, 512), bf16), VMEM((5, tok, 512), bf16),
     ]
     scratch += [VMEM((2,) + ((r // 2, c)), bf16) for r, c in pieces]
+    scratch += [VMEM(pieces[3], bf16)] * 2
     scratch += [
-        VMEM((8, wide), f32), VMEM((8, n_fc), f32), VMEM((7, 8, tok), f32), VMEM((7, 16, 512), f32),
-        pltpu.SemaphoreType.DMA((96,)), pltpu.SemaphoreType.DMA((96,)),
+        VMEM((2, tok, 128), f32),
+        VMEM((8, wide), f32), VMEM((8, n_fc), f32), VMEM((7, 8, tok), f32), VMEM((9, 16, 512), f32),
+        pltpu.SemaphoreType.DMA((128,)), pltpu.SemaphoreType.DMA((128,)),
         pltpu.SemaphoreType.DMA((64,)), pltpu.SemaphoreType.DMA((2,)),
     ]
     return pl.pallas_call(
         block_kernel,
         name="block",
         out_shape=outs,
-        in_specs=[any_spec] * 2 + [vmem] * 4 + [any_spec] * 4 + [vmem] * 3,
-        out_specs=[any_spec] * 19 + [vmem] * 2,
+        in_specs=[any_spec] * 7 + [vmem] * 8,
+        out_specs=[any_spec] * len(outs),
         scratch_shapes=scratch,
         compiler_params=pltpu.CompilerParams(
             collective_id=1, has_side_effects=True, vmem_limit_bytes=67043328
@@ -1080,12 +1192,67 @@
     half_rot = ROT // 2
     frequency = (10000.0 ** (-np.arange(half_rot, dtype=np.float32) * (2.0 / ROT))).astype(np.float32)
     angles = np.arange(length, dtype=np.float32)[:, None] * frequency[None, :]
-    tables = np.zeros((3, length, 128), np.float32)
+    tables = np.zeros((2, length, 128), np.float32)
     tables[0] = 1.0
     tables[0, :, :half_rot] = tables[0, :, half_rot:ROT] = np.cos(angles)
     tables[1, :, :half_rot] = -np.sin(angles)
-    tables[2, :, half_rot:ROT] = np.sin(angles)
+    tables[1, :, half_rot:ROT] = np.sin(angles)
     return tables
+
+
+def close_kernel(cuts, *refs):
+    count = len(cuts)
+    sources, small = refs[:count], refs[count]
+    outs, vectors = refs[count + 1 : 2 * count + 1], refs[2 * count + 1 : 2 * count + 9]
+    lows, wides = refs[2 * count + 9 : 3 * count + 9], refs[3 * count + 9 : -2]
+    in_sems, out_sems = refs[-2:]
+    loads, stores = [], []
+    for n, cut in enumerate(cuts):
+        rows = sources[n].shape[0] // cut
+        for part in range(cut):
+            at = pl.ds(part * rows, rows)
+            number = len(loads)
+            wide = lows[n] if n >= len(wides) else wides[n]
+            loads.append(
+                pltpu.make_async_copy(sources[n].at[at, :], lows[n].at[at, :], in_sems.at[number])
+            )
+            stores.append(
+                (n, at, pltpu.make_async_copy(wide.at[at, :], outs[n].at[at, :], out_sems.at[number]))
+            )
+    for copy in loads:
+        copy.start()
+    for row, (vector, length) in zip((0, 1, 2, 3, 4, 7, 11, 11), ((v, v.shape[0]) for v in vectors)):
+        for n in range(length // 512):
+            vector[n * 512 : n * 512 + 512] = small[row + n, :]
+    for load, (n, at, store) in zip(loads, stores):
+        load.wait()
+        if n < len(wides):
+            wides[n][at, :] = lows[n][at, :].astype(f32)
+        store.start()
+    for _, _, store in stores:
+        store.wait()
+
+
+def call_close(proj, qkv, fc, dense, block, grad, small):
+    any_spec = pl.BlockSpec(memory_space=pl.ANY)
+    vmem = pl.BlockSpec(memory_space=VMEM)
+    shape = jax.ShapeDtypeStruct
+    arrays = (fc, proj, qkv, dense, block, grad)
+    cuts = (4, 4, 2, 1, 2, 2)
+    outs = [shape(a.shape, f32) for a in arrays]
+    lengths = [512] * 4 + [qkv.shape[1], fc.shape[1], 512, 512]
+    outs += [shape((length,), f32) for length in lengths]
+    return pl.pallas_call(
+        functools.partial(close_kernel, cuts),
+        name="close",
+        out_shape=outs,
+        in_specs=[any_spec] * 6 + [vmem],
+        out_specs=[any_spec] * 6 + [vmem] * 8,
+        scratch_shapes=[VMEM(a.shape, a.dtype) for a in arrays]
+        + [VMEM(a.shape, f32) for a in arrays[:4]]
+        + [pltpu.SemaphoreType.DMA((sum(cuts),)), pltpu.SemaphoreType.DMA((sum(cuts),))],
+        compiler_params=pltpu.CompilerParams(vmem_limit_bytes=60 << 20),
+    )(*arrays, small)
 
 
 def fused_shards(
@@ -1093,20 +1260,14 @@
     w_qkv, b_qkv, w_dense, b_dense, w_fc, b_fc, w_proj, b_proj,
 ):
     results = call_block(
-        block_input, out_grad, ln1_gain, ln1_bias, ln2_gain, ln2_bias,
-        w_qkv, w_dense, w_fc, w_proj, b_qkv, b_fc, turn_tables(SEQ),
-    )
-    proj_total, qkv_total, fc_total, dense_total = (part.astype(f32) for part in results[:4])
-    branch, hat_grad = results[4:6]
-    stats, small = results[19:]
-    mu, rstd, total, cross = (stats[:, n : n + 1] for n in range(4))
-    block_output = block_input + branch + (b_dense + b_proj)
-    x_hat = (block_input - mu) * rstd
-    input_grad = out_grad + rstd * (hat_grad - total * (1.0 / D) - x_hat * (cross * (1.0 / D)))
+        block_input, out_grad, w_qkv, w_dense, w_fc, w_proj, turn_tables(SEQ),
+        ln1_gain, ln1_bias, ln2_gain, ln2_bias, b_qkv, b_fc, b_dense, b_proj,
+    )
+    fc, proj, qkv, dense, block, grad, *vectors = call_close(*results[:7])
+    gain_1, shift_1, gain_2, shift_2, qkv_bias, fc_bias, dense_bias, proj_bias = vectors
     return (
-        block_output, input_grad, small[0], small[1], small[2], small[3],
-        qkv_total, small[4:7].reshape(-1), dense_total, small[11],
-        fc_total, small[7:11].reshape(-1), proj_total, small[11],
+        block, grad, gain_1, shift_1, gain_2, shift_2, qkv, qkv_bias, dense, dense_bias,
+        fc, fc_bias, proj, proj_bias,
     )
 
 

time: 245 us -> 232 us (0.947)
  other arithmetic: 15 us -> 0 us
  Pallas kernels: 225 us -> 231 us
    pallas_call x0 -> x1, Pallas kernels: none -> 9.06 us  [call_close(): pl.pallas_call(functools.partial(close_kernel, cuts), name='close', out_s...]
    convert_element_type x4 -> x0, other arithmetic: 8.32 us -> none  [fused_shards(): part.astype(f32)]
    add x2 -> x0, other arithmetic: 4.69 us -> none  [the longest x1 3.99 us: fused_shards(): out_grad + rstd * (hat_grad - total * (1.0 / D) - x_hat * (cross * (1.0 /...]
    pallas_call x1, Pallas kernels: 225 us -> 222 us  [call_block(): pl.pallas_call(block_kernel, name='block', out_shape=outs, in_specs=[any_...]
where the time goes in v3:
time: 232 us; the launch traced here: 231 us
  Pallas kernels  231 us (100%)
    pallas_call x1, Pallas kernels, call_block(): pl.pallas_call(block_kernel, name='block', out_shape=outs, in_specs=[any_...  222 us
    pallas_call x1, Pallas kernels, call_close(): pl.pallas_call(functools.partial(close_kernel, cuts), name='close', out_s...  9.06 us

profile of v3, /device:TPU:1, one launch (start us, length us, event | category | flops | bytes accessed | tf_op | source)
XLA Modules:
  0.0 231.5 jit_solution(6367556895575634026)
XLA Ops:
  0.7 221.6 %block.1 = (bf16[2048,512]{1,0:T(8,128)(2,1)}, bf16[512,1536]{1,0:T(8,128)(2,1)}, bf16[512,2048]{1,0:T(8,128)(2,1)}, bf16[512,512]{1,0:T(8,128)(2,1)}, f32[512,5...) custom-call(f32[512,512]{1,0:T(8,128)} %x.1, ...), custom_call_target="tpu_custom_call" | custom-call | tf_op jit(solution)/shard_map/block/pallas_call | solution.py:1178
  222.2 9.1 %close.1 = (f32[512,2048]{1,0:T(8,128)}, f32[2048,512]{1,0:T(8,128)}, f32[512,1536]{1,0:T(8,128)}, f32[512,512]{1,0:T(8,128)}, f32[512,512]{1,0:T(8,128)}, /*ind...) custom-call(bf16[512,2048]{1,0:T(8,128)(2,1)} %get-tuple-element.35., ...), custom_call_target="tpu_custom_call" | custom-call | tf_op jit(solution)/shard_map/close/pallas_call | solution.py:1245

commit v4 on v3

--- a/solution.py
+++ b/solution.py
@@ -531,10 +531,10 @@
                 )
             )
 
-    def start(self):
+    def start(self, first, last):
         @pl.when(jnp.logical_not(self.net.middle))
         def _():
-            for copy in self.copies[:3]:
+            for copy in self.copies[first:last]:
                 copy.start()
 
     def step(self, number):
@@ -685,34 +685,40 @@
         for copy in self.loads:
             copy.wait()
         tile = 64
-
-        def add(n, _):
-            at = span(n * tile, tile)
-            parts = [buffer[at, :].astype(f32) for buffer in buffers[:3]]
-            buffers[3][at, :] = (parts[0] + parts[1] + parts[2]).astype(bf16)
-            return 0
-
-        lax.fori_loop(0, self.near.shape[0] // tile, add, 0)
-        if self.by_rows:
-            place = out.at[span(net.k * Q, Q), :]
-        else:
-            place = out.at[:, span(net.k * Q, Q)]
-        self.here = net.local(buffers[3], place)
-        self.there = net.remote(buffers[3], place, net.core)
+        self.here, self.there = [], []
+        for half in range(2):
+
+            def add(n, _, half=half):
+                at = span(half * self.depth + n * tile, tile)
+                parts = [buffer[at, :].astype(f32) for buffer in buffers[:3]]
+                buffers[3][at, :] = (parts[0] + parts[1] + parts[2]).astype(bf16)
+                return 0
+
+            lax.fori_loop(0, self.depth // tile, add, 0)
+            source = buffers[3].at[self.rows(half), :]
+            if self.by_rows:
+                place = out.at[span(net.k * Q + half * self.depth, self.depth), :]
+            else:
+                place = out.at[self.rows(half), span(net.k * Q, Q)]
+            self.here.append(net.local(source, place))
+            self.there.append(net.remote(source, place, net.core))
 
     def done(self):
-        self.here.wait()
-        self.there.wait_recv()
+        for copy in self.here:
+            copy.wait()
+        for copy in self.there:
+            copy.wait_recv()
 
 
 def block_kernel(
     x, og, w_qkv, w_dense, w_fc, w_proj, t_turn,
-    gain_1, bias_1, gain_2, bias_2, b_qkv, b_fc, b_dense, b_proj,
+    i_gain_1, i_bias_1, i_gain_2, i_bias_2, i_b_qkv, i_b_fc, i_b_dense, i_b_proj,
     o_proj, o_qkv, o_fc, o_dense, o_block, o_input, o_small,
     all_proj, r_proj, r_qkv, r_fc, r_dense, n_proj, f_proj, n_qkv, f_qkv, n_fc, f_fc,
     g_qkv, g_dense, g_fc, g_tail, xs, ys, pks, stats, rows, h1c, h1s, h2c, h2s, dyc, dys, xh,
     qb, kb, vb, probs, probs_low, oc, dob, dqc, gc, slope, dabt, stage,
     out_recv, hat_recv, j_proj, j_qkv, j_fc, j_dense, n_dense, f_dense, tables, vecs, bias, packs, small,
+    gain_1, bias_1, gain_2, bias_2, b_qkv, b_fc, b_dense, b_proj,
     send_sems, recv_sems, local_sems, stage_sems,
 ):
     tok = x.shape[0]
@@ -728,6 +734,11 @@
     qkv.send_own()
     dense.send_own()
     load_x = net.local(x, probs.at[0])
+    vectors = [
+        net.local(i_gain_1, gain_1), net.local(i_bias_1, bias_1), net.local(i_gain_2, gain_2),
+        net.local(i_bias_2, bias_2), net.local(i_b_qkv, b_qkv), net.local(i_b_fc, b_fc),
+        net.local(i_b_dense, b_dense), net.local(i_b_proj, b_proj),
+    ]
     load_og = net.local(og, probs.at[1])
     load_turn = net.local(t_turn, tables)
     tiles = Tiles(stage, stage_sems)
@@ -749,6 +760,8 @@
 
     lax.fori_loop(0, tok // step, local_norm, 0)
     pks[0] = stats[...].T[0:8]
+    for copy in vectors:
+        copy.wait()
     for n, vector in enumerate((gain_1, bias_1, gain_2, bias_2)):
         pks[0, 2 + n : 3 + n, :] = vector[...].reshape(1, 512)
     packed = [net.remote(pks.at[0], pks.at[j], net.z[j]) for j in (1, 2, 3)]
@@ -798,8 +811,9 @@
     y_line.start()
     dense.swap_near()
     qkv.swap_far()
-    dense.swap_far()
     x_line.ready()
+    fc.forward()
+    proj.send_own()
 
     for s in range(2):
         for j in range(4):
@@ -821,8 +835,6 @@
             lax.fori_loop(0, tok // step, norm, 0)
     swap_h1 = net.remote(h1s, h1c.at[theirs, :], net.core)
     swap_h2 = net.remote(h2s, h2c.at[theirs, :], net.core)
-    fc.forward()
-    proj.send_own()
     y_line.step(0)
     load_turn.wait()
     qkv.ready()
@@ -860,6 +872,7 @@
 
     lax.fori_loop(0, heads * chunks, attend, 0)
     swap_o = net.remote(oc.at[mine, :], oc.at[theirs, :], net.core)
+    dense.swap_far()
     fc.swap_near()
     y_line.step(2)
     fc.swap_far()
@@ -874,9 +887,10 @@
         slope[:, cols] = (rise + a * 0.3989422804014327 * jnp.exp(-0.5 * a * a)).astype(bf16)
         return 0
 
-    lax.fori_loop(0, width // 512, expand, 0)
+    lax.fori_loop(0, width // 1024, expand, 0)
+    proj.forward()
+    lax.fori_loop(width // 1024, width // 512, expand, 0)
     swap_g = net.remote(gc.at[mine, :], gc.at[theirs, :], net.core)
-    proj.forward()
     y_line.ready()
     for s in range(2):
         for j in range(4):
@@ -937,6 +951,7 @@
         return 0
 
     lax.fori_loop(0, heads, attend_back, 0)
+    proj.swap_far()
     swap_dq = net.remote(dqc.at[mine, :], dqc.at[theirs, :], net.core)
     net.sent(swap_h1)
     net.sent(swap_h2)
@@ -952,7 +967,6 @@
 
         lax.fori_loop(0, HALF // 512, back_first, 0)
 
-    proj.swap_far()
     proj.ready()
     qkv.release()
     loads = [
@@ -1002,7 +1016,7 @@
     lax.fori_loop(0, 6, project_head, 0)
     lax.fori_loop(0, 2, project_tail, 0)
     out_fold = Fold(net, xs, out_recv)
-    out_fold.start()
+    out_fold.start(0, 2)
 
     def back_fc(n, _):
         cols = span(n * 512, 512)
@@ -1050,7 +1064,9 @@
         packs[j, 6:8, :] = jnp.zeros((2, tok), f32)
     pack_copies = [net.remote(packs.at[j], packs.at[3 + j], net.z[j]) for j in (1, 2, 3)]
     hat_fold = Fold(net, ys, hat_recv)
-    hat_fold.start()
+    hat_fold.start(0, 2)
+    out_fold.start(2, 3)
+    hat_fold.start(2, 3)
     out_fold.step(0)
     swap_h2.wait_recv()
     swap_da.wait_recv()
@@ -1088,17 +1104,17 @@
     reload_x = net.local(x, probs.at[1])
     red_proj.prepare([g_qkv.at[:, pl.ds(n * Q, Q)] for n in range(4)])
     red_proj.finish(o_proj)
-    reload_x.wait()
-
-    def close_out(at, value):
-        probs[0, at, :] = probs[1, at, :] + value + bias[5:6, 0:512]
-
-    out_fold.total(close_out)
-    keep_block = net.local(probs.at[0], o_block)
     hat_fold.step(0)
     red_fc.join([g_fc.at[pl.ds(6 * Q + n * (Q // 2), Q // 2), :] for n in range(2)])
     hat_fold.step(1)
     hat_fold.step(2)
+    reload_x.wait()
+
+    def close_out(at, value):
+        probs[0, at, :] = probs[1, at, :] + value + bias[5:6, 0:512]
+
+    out_fold.total(close_out)
+    keep_block = net.local(probs.at[0], o_block)
     keep_block.wait()
     reload_og = net.local(og, probs.at[0])
     red_qkv.prepare([strips(0, n, 6 * Q) for n in range(4)])
@@ -1141,7 +1157,6 @@
     heads = n_attn // HD
     wide = 2 * HALF
     any_spec = pl.BlockSpec(memory_space=pl.ANY)
-    vmem = pl.BlockSpec(memory_space=VMEM)
     shape = jax.ShapeDtypeStruct
     pieces = ((n_fc, Q), (Q, n_qkv), (Q, n_fc), (n_attn, Q))
     outs = [
@@ -1172,6 +1187,8 @@
     scratch += [
         VMEM((2, tok, 128), f32),
         VMEM((8, wide), f32), VMEM((8, n_fc), f32), VMEM((7, 8, tok), f32), VMEM((9, 16, 512), f32),
+        VMEM((512,), f32), VMEM((512,), f32), VMEM((512,), f32), VMEM((512,), f32),
+        VMEM((n_qkv,), f32), VMEM((n_fc,), f32), VMEM((512,), f32), VMEM((512,), f32),
         pltpu.SemaphoreType.DMA((128,)), pltpu.SemaphoreType.DMA((128,)),
         pltpu.SemaphoreType.DMA((64,)), pltpu.SemaphoreType.DMA((2,)),
     ]
@@ -1179,7 +1196,7 @@
         block_kernel,
         name="block",
         out_shape=outs,
-        in_specs=[any_spec] * 7 + [vmem] * 8,
+        in_specs=[any_spec] * 15,
         out_specs=[any_spec] * len(outs),
         scratch_shapes=scratch,
         compiler_params=pltpu.CompilerParams(
@@ -1202,40 +1219,50 @@
 
 def close_kernel(cuts, *refs):
     count = len(cuts)
-    sources, small = refs[:count], refs[count]
-    outs, vectors = refs[count + 1 : 2 * count + 1], refs[2 * count + 1 : 2 * count + 9]
-    lows, wides = refs[2 * count + 9 : 3 * count + 9], refs[3 * count + 9 : -2]
-    in_sems, out_sems = refs[-2:]
+    refs = list(refs)
+    sources, small = [refs.pop(0) for _ in cuts], refs.pop(0)
+    outs, vectors = [refs.pop(0) for _ in cuts], [refs.pop(0) for _ in range(8)]
+    lows, sums = [refs.pop(0) for _ in cuts], refs.pop(0)
+    wides, lines = [refs.pop(0) for _ in range(4)], [refs.pop(0) for _ in range(8)]
+    in_sems, out_sems = refs
     loads, stores = [], []
     for n, cut in enumerate(cuts):
         rows = sources[n].shape[0] // cut
         for part in range(cut):
             at = pl.ds(part * rows, rows)
             number = len(loads)
-            wide = lows[n] if n >= len(wides) else wides[n]
+            wide = wides[n] if n < len(wides) else lows[n]
             loads.append(
                 pltpu.make_async_copy(sources[n].at[at, :], lows[n].at[at, :], in_sems.at[number])
             )
             stores.append(
                 (n, at, pltpu.make_async_copy(wide.at[at, :], outs[n].at[at, :], out_sems.at[number]))
             )
+    total = len(loads)
+    load_small = pltpu.make_async_copy(small, sums, in_sems.at[total])
     for copy in loads:
         copy.start()
-    for row, (vector, length) in zip((0, 1, 2, 3, 4, 7, 11, 11), ((v, v.shape[0]) for v in vectors)):
-        for n in range(length // 512):
-            vector[n * 512 : n * 512 + 512] = small[row + n, :]
+    load_small.start()
     for load, (n, at, store) in zip(loads, stores):
         load.wait()
         if n < len(wides):
             wides[n][at, :] = lows[n][at, :].astype(f32)
         store.start()
+    load_small.wait()
+    last = []
+    for n, (row, line, vector) in enumerate(zip((0, 1, 2, 3, 4, 7, 11, 11), lines, vectors)):
+        for part in range(line.shape[0] // 512):
+            line[part * 512 : part * 512 + 512] = sums[row + part, :]
+        last.append(pltpu.make_async_copy(line, vector, out_sems.at[total + n]))
+        last[-1].start()
     for _, _, store in stores:
         store.wait()
+    for copy in last:
+        copy.wait()
 
 
 def call_close(proj, qkv, fc, dense, block, grad, small):
     any_spec = pl.BlockSpec(memory_space=pl.ANY)
-    vmem = pl.BlockSpec(memory_space=VMEM)
     shape = jax.ShapeDtypeStruct
     arrays = (fc, proj, qkv, dense, block, grad)
     cuts = (4, 4, 2, 1, 2, 2)
@@ -1246,11 +1273,12 @@
         functools.partial(close_kernel, cuts),
         name="close",
         out_shape=outs,
-        in_specs=[any_spec] * 6 + [vmem],
-        out_specs=[any_spec] * 6 + [vmem] * 8,
-        scratch_shapes=[VMEM(a.shape, a.dtype) for a in arrays]
+        in_specs=[any_spec] * 7,
+        out_specs=[any_spec] * 14,
+        scratch_shapes=[VMEM(a.shape, a.dtype) for a in (*arrays, small)]
         + [VMEM(a.shape, f32) for a in arrays[:4]]
-        + [pltpu.SemaphoreType.DMA((sum(cuts),)), pltpu.SemaphoreType.DMA((sum(cuts),))],
+        + [VMEM((length,), f32) for length in lengths]
+        + [pltpu.SemaphoreType.DMA((sum(cuts) + 8,)), pltpu.SemaphoreType.DMA((sum(cuts) + 8,))],
         compiler_params=pltpu.CompilerParams(vmem_limit_bytes=60 << 20),
     )(*arrays, small)
 

time: 232 us -> 227 us (0.978)
  Pallas kernels: 231 us -> 226 us
    pallas_call x1, Pallas kernels: 222 us -> 218 us  [call_block(): pl.pallas_call(block_kernel, name='block', out_shape=outs, in_specs=[any_...]
where the time goes in v4:
time: 227 us
  Pallas kernels  226 us (100%)
    pallas_call x1, Pallas kernels, call_block(): pl.pallas_call(block_kernel, name='block', out_shape=outs, in_specs=[any_...  218 us
    pallas_call x1, Pallas kernels, call_close(): pl.pallas_call(functools.partial(close_kernel, cuts), name='close', out_s...  7.84 us

profile of v4, /device:TPU:1, one launch (start us, length us, event | category | flops | bytes accessed | tf_op | source)
XLA Modules:
  0.0 226.6 jit_solution(8907283933810516040)
XLA Ops:
  0.7 217.9 %block.1 = (bf16[2048,512]{1,0:T(8,128)(2,1)}, bf16[512,1536]{1,0:T(8,128)(2,1)}, bf16[512,2048]{1,0:T(8,128)(2,1)}, bf16[512,512]{1,0:T(8,128)(2,1)}, f32[512,5...) custom-call(f32[512,512]{1,0:T(8,128)} %x.1, ...), custom_call_target="tpu_custom_call" | custom-call | tf_op jit(solution)/shard_map/block/pallas_call | solution.py:1195
  218.6 7.8 %close.1 = (f32[512,2048]{1,0:T(8,128)}, f32[2048,512]{1,0:T(8,128)}, f32[512,1536]{1,0:T(8,128)}, f32[512,512]{1,0:T(8,128)}, f32[512,512]{1,0:T(8,128)}, /*ind...) custom-call(bf16[512,2048]{1,0:T(8,128)(2,1)} %get-tuple-element.35., ...), custom_call_target="tpu_custom_call" | custom-call | tf_op jit(solution)/shard_map/close/pallas_call | solution.py:1272

commit v5 on v4

--- a/solution.py
+++ b/solution.py
@@ -349,10 +349,21 @@
 
     def barrier(self):
         sem = pltpu.get_barrier_semaphore()
-        peers = (self.core, self.x, self.y) + self.z[1:]
-        for peer in peers:
+
+        def greet(peer):
             pl.semaphore_signal(sem, inc=1, device_id=peer, device_id_type=MESH)
-        pl.semaphore_wait(sem, len(peers))
+
+        for peer in (self.x, self.y, self.core, self.z[1]):
+            greet(peer)
+
+        @pl.when(self.middle)
+        def _():
+            greet(self.z[3])
+            pl.semaphore_wait(sem, 5)
+
+        @pl.when(jnp.logical_not(self.middle))
+        def _():
+            pl.semaphore_wait(sem, 4)
 
     def slot(self):
         self.remote_count += 1
@@ -678,15 +689,19 @@
 
     def finish(self, out):
         net, buffers = self.net, self.buffers
-        for copy in (self.far_a, self.far_b):
+        last = []
+        for half, copy in enumerate((self.far_a, self.far_b)):
             copy.wait_recv()
-        if not self.in_vmem:
-            self.loads.append(net.local(self.far, buffers[2]))
+            if not self.in_vmem:
+                rows = self.rows(half)
+                last.append(net.local(self.far.at[rows, :], buffers[2].at[rows, :]))
         for copy in self.loads:
             copy.wait()
         tile = 64
         self.here, self.there = [], []
         for half in range(2):
+            if last:
+                last[half].wait()
 
             def add(n, _, half=half):
                 at = span(half * self.depth + n * tile, tile)
@@ -764,7 +779,8 @@
         copy.wait()
     for n, vector in enumerate((gain_1, bias_1, gain_2, bias_2)):
         pks[0, 2 + n : 3 + n, :] = vector[...].reshape(1, 512)
-    packed = [net.remote(pks.at[0], pks.at[j], net.z[j]) for j in (1, 2, 3)]
+    p_line = Line(net, pks)
+    p_line.start()
     for weight in (qkv, dense, fc):
         weight.place_own()
     bias[...] = jnp.zeros_like(bias)
@@ -782,8 +798,9 @@
         return 0
 
     lax.fori_loop(0, tok // step, local_grad, 0)
-    for pack in packed:
-        pack.wait_recv()
+    for hop in range(3):
+        p_line.step(hop)
+    p_line.ready()
     means = [pks[j, 0:1, :] for j in range(4)]
     mu = (means[0] + means[1] + means[2] + means[3]) * 0.25
     spread = [pks[j, 1:2, :] + (means[j] - mu) * (means[j] - mu) for j in range(4)]
@@ -1145,6 +1162,7 @@
         weight.done()
     keep_small.wait()
     keep_input.wait()
+    p_line.drain()
     out_fold.drain()
     hat_fold.drain()
     net.drain()

time: 227 us -> 225 us (level)
  no operation moved by 1% of the time
where the time goes in v5:
time: 225 us; the launch traced here: 224 us
  Pallas kernels  224 us (100%)
    pallas_call x1, Pallas kernels, call_block(): pl.pallas_call(block_kernel, name='block', out_shape=outs, in_specs=[any_...  216 us
    pallas_call x1, Pallas kernels, call_close(): pl.pallas_call(functools.partial(close_kernel, cuts), name='close', out_s...  7.84 us

profile of v5, /device:TPU:1, one launch (start us, length us, event | category | flops | bytes accessed | tf_op | source)
XLA Modules:
  0.0 224.4 jit_solution(5226461420353778332)
XLA Ops:
  0.7 215.7 %block.1 = (bf16[2048,512]{1,0:T(8,128)(2,1)}, bf16[512,1536]{1,0:T(8,128)(2,1)}, bf16[512,2048]{1,0:T(8,128)(2,1)}, bf16[512,512]{1,0:T(8,128)(2,1)}, f32[512,5...) custom-call(f32[512,512]{1,0:T(8,128)} %x.1, ...), custom_call_target="tpu_custom_call" | custom-call | tf_op jit(solution)/shard_map/block/pallas_call | solution.py:1213
  216.4 7.8 %close.1 = (f32[512,2048]{1,0:T(8,128)}, f32[2048,512]{1,0:T(8,128)}, f32[512,1536]{1,0:T(8,128)}, f32[512,512]{1,0:T(8,128)}, f32[512,512]{1,0:T(8,128)}, /*ind...) custom-call(bf16[512,2048]{1,0:T(8,128)(2,1)} %get-tuple-element.35., ...), custom_call_target="tpu_custom_call" | custom-call | tf_op jit(solution)/shard_map/close/pallas_call | solution.py:1290

commit v6 on v5

--- a/solution.py
+++ b/solution.py
@@ -1105,19 +1105,19 @@
     total = packs[0] + packs[4] + packs[5] + packs[6]
     rows[2:4, :] = total[0:2, :]
     stats[...] = rows[...].T
-    me = net.k * 4 + net.r
-    small[me, 0:4, :] = total[2:6, :]
+    small[0, 0:4, :] = total[2:6, :]
     for n in range(3):
-        small[me, 4 + n : 5 + n, :] = bias[0:1, n * 512 : n * 512 + 512]
+        small[0, 4 + n : 5 + n, :] = bias[0:1, n * 512 : n * 512 + 512]
     for n in range(4):
-        small[me, 7 + n : 8 + n, :] = bias[2:3, n * 512 : n * 512 + 512]
-    small[me, 11:12, :] = bias[1:2, 0:512]
-    small[me, 12:16, :] = jnp.zeros((4, 512), f32)
-    small_copies = []
-    for n in range(1, 8):
-        row = flip(net.r % 2, n % 2) + 2 * flip(net.r // 2, n // 2 % 2)
-        peer = (flip(net.k, n // 4), row, net.c)
-        small_copies.append(net.remote(small.at[me], small.at[me], peer))
+        small[0, 7 + n : 8 + n, :] = bias[2:3, n * 512 : n * 512 + 512]
+    small[0, 11:12, :] = bias[1:2, 0:512]
+    small[0, 12:16, :] = jnp.zeros((4, 512), f32)
+    net.remote(small.at[0], small.at[1], net.core).wait_recv()
+    own_rows = span(net.k * 8, 8)
+    small[2 + net.r, 0:8, :] = small[0, own_rows, :] + small[1, own_rows, :]
+    place = small.at[2 + net.r, pl.ds(0, 8), :]
+    across = (net.k, 3 - net.r, net.c)
+    small_copies = [net.remote(place, place, peer) for peer in (net.x, net.y, across)]
     reload_x = net.local(x, probs.at[1])
     red_proj.prepare([g_qkv.at[:, pl.ds(n * Q, Q)] for n in range(4)])
     red_proj.finish(o_proj)
@@ -1141,11 +1141,9 @@
     red_dense.prepare([g_tail.at[pl.ds(n * attn, attn), pl.ds(Q, Q)] for n in range(4)])
     for copy in small_copies:
         copy.wait_recv()
-    grand = small[0]
-    for n in range(1, 8):
-        grand = grand + small[n]
-    small[8] = grand
-    keep_small = net.local(small.at[8], o_small)
+    small[6, own_rows, :] = small[2, 0:8] + small[3, 0:8] + small[4, 0:8] + small[5, 0:8]
+    place = small.at[6, own_rows, :]
+    swap_small = net.remote(place, place, net.core)
     reload_og.wait()
 
     def close_hat(at, value):
@@ -1156,6 +1154,8 @@
 
     hat_fold.total(close_hat)
     keep_input = net.local(probs.at[0], o_input)
+    swap_small.wait_recv()
+    keep_small = net.local(small.at[6], o_small)
     red_fc.finish(o_fc)
     red_dense.finish(o_dense)
     for weight in (red_proj, red_qkv, red_fc, red_dense):
@@ -1204,7 +1204,7 @@
     scratch += [VMEM(pieces[3], bf16)] * 2
     scratch += [
         VMEM((2, tok, 128), f32),
-        VMEM((8, wide), f32), VMEM((8, n_fc), f32), VMEM((7, 8, tok), f32), VMEM((9, 16, 512), f32),
+        VMEM((8, wide), f32), VMEM((8, n_fc), f32), VMEM((7, 8, tok), f32), VMEM((7, 16, 512), f32),
         VMEM((512,), f32), VMEM((512,), f32), VMEM((512,), f32), VMEM((512,), f32),
         VMEM((n_qkv,), f32), VMEM((n_fc,), f32), VMEM((512,), f32), VMEM((512,), f32),
         pltpu.SemaphoreType.DMA((128,)), pltpu.SemaphoreType.DMA((128,)),

time: 225 us -> 223 us (level)
  Pallas kernels: 224 us -> 221 us
where the time goes in v6:
time: 223 us; the launch traced here: 222 us
  Pallas kernels  221 us (99%)
    pallas_call x1, Pallas kernels, call_block(): pl.pallas_call(block_kernel, name='block', out_shape=outs, in_specs=[any_...  214 us
    pallas_call x1, Pallas kernels, call_close(): pl.pallas_call(functools.partial(close_kernel, cuts), name='close', out_s...  7.84 us

profile of v6, /device:TPU:1, one launch (start us, length us, event | category | flops | bytes accessed | tf_op | source)
XLA Modules:
  0.0 222.2 jit_solution(9202341591569849054)
XLA Ops:
  0.7 213.6 %block.1 = (bf16[2048,512]{1,0:T(8,128)(2,1)}, bf16[512,1536]{1,0:T(8,128)(2,1)}, bf16[512,2048]{1,0:T(8,128)(2,1)}, bf16[512,512]{1,0:T(8,128)(2,1)}, f32[512,5...) custom-call(f32[512,512]{1,0:T(8,128)} %x.1, ...), custom_call_target="tpu_custom_call" | custom-call | tf_op jit(solution)/shard_map/block/pallas_call | solution.py:1213
  214.3 7.8 %close.1 = (f32[512,2048]{1,0:T(8,128)}, f32[2048,512]{1,0:T(8,128)}, f32[512,1536]{1,0:T(8,128)}, f32[512,512]{1,0:T(8,128)}, f32[512,512]{1,0:T(8,128)}, /*ind...) custom-call(bf16[512,2048]{1,0:T(8,128)(2,1)} %get-tuple-element.35., ...), custom_call_target="tpu_custom_call" | custom-call | tf_op jit(solution)/shard_map/close/pallas_call | solution.py:1290

commit v7 on v6

--- a/solution.py
+++ b/solution.py
@@ -1072,9 +1072,6 @@
     lax.fori_loop(0, 4, back_norm, 0)
 
     fc.release()
-    red_qkv.join(
-        [g_fc.at[pl.ds(7 * Q + n * (Q // 2), Q // 2), pl.ds(0, 6 * Q)] for n in range(2)]
-    )
     turned = stats[...].T
     for j in range(4):
         packs[j, 0:2, :] = turned[0:2]
@@ -1123,6 +1120,9 @@
     red_proj.finish(o_proj)
     hat_fold.step(0)
     red_fc.join([g_fc.at[pl.ds(6 * Q + n * (Q // 2), Q // 2), :] for n in range(2)])
+    red_qkv.join(
+        [g_fc.at[pl.ds(7 * Q + n * (Q // 2), Q // 2), pl.ds(0, 6 * Q)] for n in range(2)]
+    )
     hat_fold.step(1)
     hat_fold.step(2)
     reload_x.wait()
@@ -1134,10 +1134,9 @@
     keep_block = net.local(probs.at[0], o_block)
     keep_block.wait()
     reload_og = net.local(og, probs.at[0])
-    red_qkv.prepare([strips(0, n, 6 * Q) for n in range(4)])
-    red_qkv.finish(o_qkv)
     red_dense.join([g_tail.at[pl.ds(n * attn // 2, attn // 2), pl.ds(0, Q)] for n in range(2)])
     red_fc.prepare([strips(4 * Q, n, 8 * Q) for n in range(4)])
+    red_qkv.prepare([strips(0, n, 6 * Q) for n in range(4)])
     red_dense.prepare([g_tail.at[pl.ds(n * attn, attn), pl.ds(Q, Q)] for n in range(4)])
     for copy in small_copies:
         copy.wait_recv()
@@ -1157,6 +1156,7 @@
     swap_small.wait_recv()
     keep_small = net.local(small.at[6], o_small)
     red_fc.finish(o_fc)
+    red_qkv.finish(o_qkv)
     red_dense.finish(o_dense)
     for weight in (red_proj, red_qkv, red_fc, red_dense):
         weight.done()
@@ -1283,7 +1283,7 @@
     any_spec = pl.BlockSpec(memory_space=pl.ANY)
     shape = jax.ShapeDtypeStruct
     arrays = (fc, proj, qkv, dense, block, grad)
-    cuts = (4, 4, 2, 1, 2, 2)
+    cuts = (2, 2, 2, 1, 1, 1)
     outs = [shape(a.shape, f32) for a in arrays]
     lengths = [512] * 4 + [qkv.shape[1], fc.shape[1], 512, 512]
     outs += [shape((length,), f32) for length in lengths]

time: 223 us -> 222 us (level)
  no operation moved by 1% of the time
where the time goes in v7:
time: 222 us
  Pallas kernels  221 us (100%)
    pallas_call x1, Pallas kernels, call_block(): pl.pallas_call(block_kernel, name='block', out_shape=outs, in_specs=[any_...  213 us
    pallas_call x1, Pallas kernels, call_close(): pl.pallas_call(functools.partial(close_kernel, cuts), name='close', out_s...  7.59 us

profile of v7, /device:TPU:1, one launch (start us, length us, event | category | flops | bytes accessed | tf_op | source)
XLA Modules:
  0.0 221.5 jit_solution(15142988883507716624)
XLA Ops:
  0.7 213.1 %block.1 = (bf16[2048,512]{1,0:T(8,128)(2,1)}, bf16[512,1536]{1,0:T(8,128)(2,1)}, bf16[512,2048]{1,0:T(8,128)(2,1)}, bf16[512,512]{1,0:T(8,128)(2,1)}, f32[512,5...) custom-call(f32[512,512]{1,0:T(8,128)} %x.1, ...), custom_call_target="tpu_custom_call" | custom-call | tf_op jit(solution)/shard_map/block/pallas_call | solution.py:1213
  213.8 7.6 %close.1 = (f32[512,2048]{1,0:T(8,128)}, f32[2048,512]{1,0:T(8,128)}, f32[512,1536]{1,0:T(8,128)}, f32[512,512]{1,0:T(8,128)}, f32[512,512]{1,0:T(8,128)}, /*ind...) custom-call(bf16[512,2048]{1,0:T(8,128)(2,1)} %get-tuple-element.35., ...), custom_call_target="tpu_custom_call" | custom-call | tf_op jit(solution)/shard_map/close/pallas_call | solution.py:1290

commit v8 on v7

--- a/solution.py
+++ b/solution.py
@@ -689,10 +689,11 @@
 
     def finish(self, out):
         net, buffers = self.net, self.buffers
+        arrivals = (self.far_a, self.far_b)
         last = []
-        for half, copy in enumerate((self.far_a, self.far_b)):
-            copy.wait_recv()
-            if not self.in_vmem:
+        if not self.in_vmem:
+            for half, copy in enumerate(arrivals):
+                copy.wait_recv()
                 rows = self.rows(half)
                 last.append(net.local(self.far.at[rows, :], buffers[2].at[rows, :]))
         for copy in self.loads:
@@ -700,7 +701,9 @@
         tile = 64
         self.here, self.there = [], []
         for half in range(2):
-            if last:
+            if self.in_vmem:
+                arrivals[half].wait_recv()
+            else:
                 last[half].wait()
 
             def add(n, _, half=half):

time: 222 us -> 222 us (level)
  no operation moved by 1% of the time
where the time goes in v8:
time: 222 us
  Pallas kernels  221 us (100%)
    pallas_call x1, Pallas kernels, call_block(): pl.pallas_call(block_kernel, name='block', out_shape=outs, in_specs=[any_...  213 us
    pallas_call x1, Pallas kernels, call_close(): pl.pallas_call(functools.partial(close_kernel, cuts), name='close', out_s...  7.59 us

profile of v8, /device:TPU:1, one launch (start us, length us, event | category | flops | bytes accessed | tf_op | source)
XLA Modules:
  0.0 221.5 jit_solution(8891738194744617673)
XLA Ops:
  0.7 213.1 %block.1 = (bf16[2048,512]{1,0:T(8,128)(2,1)}, bf16[512,1536]{1,0:T(8,128)(2,1)}, bf16[512,2048]{1,0:T(8,128)(2,1)}, bf16[512,512]{1,0:T(8,128)(2,1)}, f32[512,5...) custom-call(f32[512,512]{1,0:T(8,128)} %x.1, ...), custom_call_target="tpu_custom_call" | custom-call | tf_op jit(solution)/shard_map/block/pallas_call | solution.py:1216
  213.8 7.6 %close.1 = (f32[512,2048]{1,0:T(8,128)}, f32[2048,512]{1,0:T(8,128)}, f32[512,1536]{1,0:T(8,128)}, f32[512,512]{1,0:T(8,128)}, f32[512,512]{1,0:T(8,128)}, /*ind...) custom-call(bf16[512,2048]{1,0:T(8,128)(2,1)} %get-tuple-element.35., ...), custom_call_target="tpu_custom_call" | custom-call | tf_op jit(solution)/shard_map/close/pallas_call | solution.py:1293

commit v9 on v7

--- a/solution.py
+++ b/solution.py
@@ -1282,8 +1282,8 @@
 def call_close(proj, qkv, fc, dense, block, grad, small):
     any_spec = pl.BlockSpec(memory_space=pl.ANY)
     shape = jax.ShapeDtypeStruct
-    arrays = (fc, proj, qkv, dense, block, grad)
-    cuts = (2, 2, 2, 1, 1, 1)
+    arrays = (dense, qkv, fc, proj, block, grad)
+    cuts = (1, 2, 2, 2, 1, 1)
     outs = [shape(a.shape, f32) for a in arrays]
     lengths = [512] * 4 + [qkv.shape[1], fc.shape[1], 512, 512]
     outs += [shape((length,), f32) for length in lengths]
@@ -1309,7 +1309,7 @@
         block_input, out_grad, w_qkv, w_dense, w_fc, w_proj, turn_tables(SEQ),
         ln1_gain, ln1_bias, ln2_gain, ln2_bias, b_qkv, b_fc, b_dense, b_proj,
     )
-    fc, proj, qkv, dense, block, grad, *vectors = call_close(*results[:7])
+    dense, qkv, fc, proj, block, grad, *vectors = call_close(*results[:7])
     gain_1, shift_1, gain_2, shift_2, qkv_bias, fc_bias, dense_bias, proj_bias = vectors
     return (
         block, grad, gain_1, shift_1, gain_2, shift_2, qkv, qkv_bias, dense, dense_bias,

time: 222 us -> 222 us (level)
  no operation moved by 1% of the time
where the time goes in v9:
time: 222 us
  Pallas kernels  221 us (100%)
    pallas_call x1, Pallas kernels, call_block(): pl.pallas_call(block_kernel, name='block', out_shape=outs, in_specs=[any_...  213 us
    pallas_call x1, Pallas kernels, call_close(): pl.pallas_call(functools.partial(close_kernel, cuts), name='close', out_s...  7.94 us

profile of v9, /device:TPU:1, one launch (start us, length us, event | category | flops | bytes accessed | tf_op | source)
XLA Modules:
  0.0 221.9 jit_solution(16149759353435324260)
XLA Ops:
  0.7 213.1 %block.1 = (bf16[2048,512]{1,0:T(8,128)(2,1)}, bf16[512,1536]{1,0:T(8,128)(2,1)}, bf16[512,2048]{1,0:T(8,128)(2,1)}, bf16[512,512]{1,0:T(8,128)(2,1)}, f32[512,5...) custom-call(f32[512,512]{1,0:T(8,128)} %x.1, ...), custom_call_target="tpu_custom_call" | custom-call | tf_op jit(solution)/shard_map/block/pallas_call | solution.py:1213
  213.8 7.9 %close.1 = (f32[512,512]{1,0:T(8,128)}, f32[512,1536]{1,0:T(8,128)}, f32[512,2048]{1,0:T(8,128)}, f32[2048,512]{1,0:T(8,128)}, f32[512,512]{1,0:T(8,128)}, /*ind...) custom-call(bf16[512,512]{1,0:T(8,128)(2,1)} %get-tuple-element.35.r, ...), custom_call_target="tpu_custom_call" | custom-call | tf_op jit(solution)/shard_map/close/pallas_call | solution.py:1290
